TPU v7x, 128 devices: a whole 4x4x4 slice. The times are simulated.
128 devices in a mesh: dp: 1, ep: 16 (over z, y), tp: 8 (over x, core).
Axes of the slice: x: 4, y: 4, z: 4, core: 2. Of those that a mesh axis runs over, the one named last changes fastest.
Arguments:
- tokens: bfloat16 [32768, 2048], P(('dp', 'ep', 'tp'))
- expert_ids: int32 [32768, 8], P(('dp', 'ep', 'tp'))
- gate_vals: float32 [32768, 8], P(('dp', 'ep', 'tp'))
- w_gate: bfloat16 [128, 2048, 768], P('ep', None, 'tp')
- w_up: bfloat16 [128, 2048, 768], P('ep', None, 'tp')
- w_down: bfloat16 [128, 768, 2048], P('ep', 'tp')
Outputs:
- output: bfloat16 [32768, 2048], P(('dp', 'ep', 'tp'))
All inputs are finite; a program needn't handle non-finite values.
Results may differ from a plain program's by a relative error of at most 0.010046.
Values are sent between devices in bfloat16 or wider.
A program may use at most 1 GiB of HBM per device.

v0:
```python
import jax
import jax.numpy as jnp
from jax import lax
from jax.sharding import PartitionSpec as P

CAP_FACTOR = 2


def slot_table(ids_loc, n_exp):
    tok_loc, n_top = ids_loc.shape
    flat_ids = ids_loc.reshape(tok_loc * n_top)
    one_hot = (flat_ids[:, None] == jnp.arange(n_exp, dtype=jnp.int32)[None, :]).astype(jnp.int32)
    preceding = jnp.cumsum(one_hot, axis=0) - one_hot
    return jnp.sum(preceding * one_hot, axis=1).reshape(tok_loc, n_top)


def dispatch_plan(ids_loc, n_exp, capacity):
    tok_loc, n_top = ids_loc.shape
    slot_ids = slot_table(ids_loc, n_exp)
    kept_mask = slot_ids < capacity
    flat_pos = jnp.where(kept_mask, ids_loc * capacity + slot_ids, n_exp * capacity)
    tok_index = jnp.broadcast_to(jnp.arange(tok_loc, dtype=jnp.int32)[:, None], (tok_loc, n_top))
    src_rows = jnp.zeros((n_exp * capacity,), jnp.int32).at[flat_pos.reshape(-1)].set(tok_index.reshape(-1), mode="drop")
    return src_rows, flat_pos, kept_mask


def combine_rows(y_slots, flat_pos, kept_mask, gate_loc):
    picked = jnp.take(y_slots, jnp.where(kept_mask, flat_pos, 0), axis=0)
    weights = jnp.where(kept_mask, gate_loc, 0.0)
    return jnp.sum(picked.astype(jnp.float32) * weights[:, :, None], axis=1)


def solution(mesh):
    expert_ranks = mesh.shape["ep"]
    row_spec = P(("dp", "ep", "tp"), None)

    def local_layer(x_loc, ids_loc, gate_loc, wg_loc, wu_loc, wd_loc):
        tok_loc, d_model = x_loc.shape
        n_top = ids_loc.shape[1]
        local_exp = wg_loc.shape[0]
        n_exp = local_exp * expert_ranks
        capacity = CAP_FACTOR * n_top * tok_loc // n_exp
        src_rows, flat_pos, kept_mask = dispatch_plan(ids_loc, n_exp, capacity)
        send_rows = jnp.take(x_loc, src_rows, axis=0).reshape(expert_ranks, local_exp, capacity, d_model)
        recv_rows = lax.all_to_all(send_rows, "ep", 0, 2, tiled=True)[0]
        group_rows = lax.all_gather(recv_rows, "tp", axis=1, tiled=True)
        gate_pre = jnp.einsum("erd,edf->erf", group_rows, wg_loc, preferred_element_type=jnp.float32)
        up_pre = jnp.einsum("erd,edf->erf", group_rows, wu_loc, preferred_element_type=jnp.float32)
        hidden = (jax.nn.silu(gate_pre) * up_pre).astype(jnp.bfloat16)
        part_sums = jnp.einsum("erf,efd->erd", hidden, wd_loc, preferred_element_type=jnp.float32).astype(jnp.bfloat16)
        pieces = lax.all_to_all(part_sums[None], "tp", 2, 0, tiled=True)
        y_rows = jnp.sum(pieces.astype(jnp.float32), axis=0).astype(jnp.bfloat16)
        returned = lax.all_to_all(y_rows[None], "ep", 2, 0, tiled=True)
        y_slots = returned.reshape(n_exp * capacity, d_model)
        return combine_rows(y_slots, flat_pos, kept_mask, gate_loc).astype(jnp.bfloat16)

    return jax.shard_map(local_layer, mesh=mesh, in_specs=(row_spec, row_spec, row_spec, P("ep", None, "tp"), P("ep", None, "tp"), P("ep", "tp", None)), out_specs=row_spec, check_vma=False)
```

profile of v0, /device:TPU:1, one launch (start us, length us, event | category | flops | bytes accessed | tf_op | source)
XLA Modules:
  0.0 2971.4 jit_solution(8347164474643526661)
XLA Ops:
  6.5 0.8 broadcast_multiply_fusion
  7.4 0.9 copy.20
  9.3 1.0 copy-done.2
  10.3 1.3 broadcast_add_fusion
  11.6 0.3 copy.23
  11.9 0.6 fusion.2
  12.8 8.1 scatter_custom_fusion
  21.0 32.7 %gather_fusion = bf16[4096,2048]{1,0:T(8,128)(2,1)} fusion(bf16[256,2048]{1,0:T(8,128)(2,1)} %param.6, s32[4096]{0:T(1024)S(1)} %fusion.6), kind=kCustom, calls=%fused_computation | custom fusion | bytes 33570816 | tf_op jit(solution)/shard_map/jit(_take)/gather | solution.py:44
  53.7 8.5 broadcast_select_fusion
  62.2 198.9 %all_to_all.42 = bf16[16,8,32,2048]{3,2,1,0:T(8,128)(2,1)S(1)} all-to-all(bf16[16,8,32,2048]{3,2,1,0:T(8,128)(2,1)S(1)} %broadcast_select_fusion), channel_id=1, replica_groups=mesh['dp'=1,'ep'=16,'tp'=8] {'ep'}, dimensions={0} | all-to-all | bytes 33554432 | tf_op jit(solution)/shard_map/all_to_all | solution.py:45
  261.1 6.6 copy.26
  267.7 590.5 %all-gather.2.cloned.1.call-done = bf16[8,4096,2048]{2,1,0:T(8,128)(2,1)} async-done(((bf16[8,512,2048]{2,1,0:T(8,128)(2,1)}), bf16[8,4096,2048]{2,1,0:T(8,128)(2,1)}) %all-gather.2.cloned.1.call-update) | async-done | bytes 134217744 | tf_op jit(solution)/shard_map/all_gather | solution.py:46
  858.1 54.9 %fusion.10 = f32[8,4096,96]{1,2,0:T(8,128)} fusion(bf16[8,4096,2048]{2,1,0:T(8,128)(2,1)} %all-gather.2.cloned.1.call-done, bf16[8,2048,96]{1,2,0:T(8,128)(2,1)} %param.9), kind=kOutput, calls=%fused_computation.33 | convolution fusion | flops 12884901888 | bytes 149946368 | tf_op jit(solution)/shard_map/erd,edf->erf/dot_general | solution.py:47
  913.0 55.0 %multiply_convert_fusion.clone.4 = bf16[8,4096,96]{1,2,0:T(8,128)(2,1)} fusion(f32[8,4096,96]{1,2,0:T(8,128)} %fusion.10, bf16[8,4096,2048]{2,1,0:T(8,128)(2,1)} %all-gather.2.cloned.1.call-done, bf16[8,2048,96]{1,2,0:T(8,128)(2,1)} %param.10), kind=kOutput, calls=%fused_computation.6.clone.clone.clone.1 | convolution fusion | flops 12903776256 | bytes 156237824 | tf_op jit(solution)/shard_map/erd,edf->erf/dot_general | solution.py:48
  968.0 51.5 %convert_bitcast_fusion = bf16[1,8,4096,2048]{3,2,1,0:T(8,128)(2,1)} fusion(bf16[8,96,2048]{2,1,0:T(8,128)(2,1)S(1)} %copy-done, bf16[8,4096,96]{1,2,0:T(8,128)(2,1)} %multiply_convert_fusion.clone.4), kind=kOutput, calls=%fused_computation.3 | convolution fusion | flops 12952010752 | bytes 143654912 | tf_op jit(solution)/shard_map/erf,efd->erd/dot_general | solution.py:50
  1019.5 111.6 %copy.27 = bf16[1,8,4096,2048]{3,1,0,2:T(8,128)(2,1)} copy(bf16[1,8,4096,2048]{3,2,1,0:T(8,128)(2,1)} %convert_bitcast_fusion) | data formatting | bytes 268435456 | tf_op jit(solution)/shard_map/broadcast_in_dim | solution.py:51
  1131.1 1474.4 %all_to_all.43 = bf16[1,8,4096,2048]{3,1,0,2:T(8,128)(2,1)} all-to-all(bf16[1,8,4096,2048]{3,1,0,2:T(8,128)(2,1)} %copy.27), channel_id=1, replica_groups=mesh['dp'=1,'ep'=16,'tp'=8] {'tp'}, dimensions={2} | all-to-all | bytes 268435456 | tf_op jit(solution)/shard_map/all_to_all | solution.py:51
  2605.5 50.1 %reduce_sum.31 = bf16[8,512,2048]{2,0,1:T(8,128)(2,1)} reduce(bf16[8,8,512,2048]{3,0,2,1:T(8,128)(2,1)} %bitcast.9, bf16[]{:T(256)} %constant.46.clone.1), dimensions={1}, to_apply=%region_4.5 | reduce | flops 58720256 | bytes 150994944 | tf_op jit(solution)/shard_map/reduce_sum | solution.py:52
  2655.6 6.9 all-to-all-start.2
  2662.9 245.3 %all-to-all-done.2 = bf16[1,8,512,2048]{3,1,0,2:T(8,128)(2,1)} async-done(((bf16[1,8,512,2048]{3,1,0,2:T(8,128)(2,1)}), bf16[1,8,512,2048]{3,1,0,2:T(8,128)(2,1)}, u32[]{:S(2)}, u32[]{:S(2)}) %all-to-all-start.2) | async-done | bytes 16777248 | tf_op jit(solution)/shard_map/all_to_all | solution.py:53
  2908.2 15.1 copy.28
  2923.2 6.6 copy.29
  2929.8 24.4 gather_fusion.1
  2954.3 10.3 multiply_reduce_fusion
  (39 shorter events, 1.7 us)
Async XLA Ops:
  6.5 961.5 %copy-start = (bf16[8,96,2048]{2,1,0:T(8,128)(2,1)S(1)}, bf16[8,96,2048]{2,1,0:T(8,128)(2,1)}, u32[]{:S(2)}) copy-start(bf16[8,96,2048]{2,1,0:T(8,128)(2,1)} %param.11) | copy-start | bytes 9437188
  6.5 851.6 %all-gather.2.cloned.1.call-start = ((), (), s32[]{:S(2)}) async-start(), calls=%async_computation.3 | async-start | bytes 150994944 | tf_op jit(solution)/shard_map/all_gather | solution.py:46
  8.7 45.0 %copy-start.5 = (s32[256,8]{1,0:T(8,128)}, s32[256,8]{1,0:T(8,128)S(1)}, u32[]{:S(2)}) copy-start(s32[256,8]{1,0:T(8,128)S(1)} %copy.25) | copy-start | bytes 24580
  9.3 1.0 copy-start.2
  12.7 41.1 %copy-start.3 = (s32[256,8]{1,0:T(8,128)}, s32[256,8]{1,0:T(8,128)S(1)}, u32[]{:S(2)}) copy-start(s32[256,8]{1,0:T(8,128)S(1)} %reshape.79) | copy-start | bytes 24580
  2655.6 6.9 copy-start.7
  2655.6 7.0 copy-start.4
  2655.6 7.0 copy-start.6
  2655.6 252.5 %all-to-all-start.2 = ((bf16[1,8,512,2048]{3,1,0,2:T(8,128)(2,1)}), bf16[1,8,512,2048]{3,1,0,2:T(8,128)(2,1)}, u32[]{:S(2)}, u32[]{:S(2)}) async-start(bf16[1,8,512,2048]{3,1,0,2:T(8,128)(2,1)} %bitcast.44), calls=%async_computation.2 | async-start | bytes 33554432 | tf_op jit(solution)/shard_map/all_to_all | solution.py:53
  2929.8 34.8 %copy-start.1 = (bf16[8,96,2048]{2,1,0:T(8,128)(2,1)S(1)}, bf16[8,96,2048]{2,1,0:T(8,128)(2,1)}, u32[]{:S(2)}) copy-start(bf16[8,96,2048]{2,1,0:T(8,128)(2,1)} %param.11) | copy-start | bytes 9437188
Sparse Core Ops, SparseCore 0:
  267.8 590.2 all-gather.1
where the time goes:
time: 2970 us
  blocking collectives  1670 us (56%)
  waiting for transfers between devices  836 us (28%)
  local copies, waits for them, and re-layouts  208 us (7%)
  matrix products  161 us (5%)
  other arithmetic  72.2 us (2%)
    all_to_all x1, blocking collectives, local_layer(): pieces = lax.all_to_all(part_sums[None], 'tp', 2, 0, tiled=True)  1470 us
    all_gather x1, waiting for transfers between devices, local_layer(): group_rows = lax.all_gather(recv_rows, 'tp', axis=1, tiled=True)  590 us
    all_to_all x1, waiting for transfers between devices, local_layer(): returned = lax.all_to_all(y_rows[None], 'ep', 2, 0, tiled=True)  245 us
    all_to_all x1, blocking collectives, local_layer(): recv_rows = lax.all_to_all(send_rows, 'ep', 0, 2, tiled=True)[0]  199 us
    broadcast_in_dim x1, local copies, waits for them, and re-layouts, local_layer(): pieces = lax.all_to_all(part_sums[None], 'tp', 2, 0, tiled=True)  112 us
  transfers between devices with their start and end apart: 2, of which 2 were waited for; matrix products, arithmetic and copies ran while one was open for 0% of the time, Pallas kernels for 0%

commit v1 on v0

v1 whole, which is shorter than its diff:
```python
import jax
import jax.numpy as jnp
from jax import lax
from jax.sharding import PartitionSpec as P

CAP_FACTOR = 2


def slot_map(ids_loc, gate_loc, n_exp, capacity):
    tok_loc = ids_loc.shape[0]
    hit = ids_loc[None, :, :] == jnp.arange(n_exp, dtype=jnp.int32)[:, None, None]
    chosen = jnp.any(hit, axis=2)
    gates = jnp.sum(jnp.where(hit, gate_loc[None], 0.0), axis=2)
    before = (jnp.arange(tok_loc)[:, None] < jnp.arange(tok_loc)[None, :]).astype(jnp.bfloat16)
    slots = jnp.dot(chosen.astype(jnp.bfloat16), before, preferred_element_type=jnp.float32)
    slots = jnp.where(chosen & (slots < capacity), slots, -1.0)
    return slots, gates


def split3(g):
    hi = lax.reduce_precision(g, 8, 7)
    mid = lax.reduce_precision(g - hi, 8, 7)
    lo = g - hi - mid
    return [v.astype(jnp.bfloat16) for v in (hi, mid, lo)]


def solution(mesh):
    expert_ranks = mesh.shape["ep"]
    row_spec = P(("dp", "ep", "tp"), None)

    def local_layer(x_loc, ids_loc, gate_loc, wg_loc, wu_loc, wd_loc):
        tok_loc, d_model = x_loc.shape
        n_top = ids_loc.shape[1]
        local_exp = wg_loc.shape[0]
        n_exp = local_exp * expert_ranks
        capacity = CAP_FACTOR * n_top * tok_loc // n_exp
        wgt = lax.all_gather(jnp.swapaxes(wg_loc, 1, 2), "tp")
        wut = lax.all_gather(jnp.swapaxes(wu_loc, 1, 2), "tp")
        wdt = lax.all_gather(wd_loc, "tp")
        slots, gates = slot_map(ids_loc, gate_loc, n_exp, capacity)
        tok_all = lax.all_gather(x_loc, "ep")
        meta = lax.all_to_all(slots.reshape(expert_ranks, local_exp, tok_loc), "ep", 0, 0, tiled=True)
        cap_iota = jnp.arange(capacity, dtype=jnp.float32)
        pick = (meta[:, :, None, :] == cap_iota[None, None, :, None]).astype(jnp.bfloat16)
        rows = jnp.einsum("sect,std->escd", pick, tok_all, preferred_element_type=jnp.float32).astype(jnp.bfloat16)
        rows = rows.reshape(local_exp, expert_ranks * capacity, d_model)
        gate_pre = jnp.einsum("erd,tefd->ertf", rows, wgt, preferred_element_type=jnp.float32)
        up_pre = jnp.einsum("erd,tefd->ertf", rows, wut, preferred_element_type=jnp.float32)
        hidden = (jax.nn.silu(gate_pre) * up_pre).astype(jnp.bfloat16)
        y_rows = jnp.einsum("ertf,tefd->erd", hidden, wdt, preferred_element_type=jnp.float32).astype(jnp.bfloat16)
        y_rows = y_rows.reshape(local_exp, expert_ranks, capacity, d_model)
        returned = lax.all_to_all(y_rows, "ep", 1, 1, tiled=True)
        mine = slots.reshape(expert_ranks, local_exp, tok_loc)
        place = mine[:, :, None, :] == cap_iota[None, None, :, None]
        acc = 0.0
        for part in split3(gates.reshape(expert_ranks, local_exp, tok_loc)):
            wts = jnp.where(place, part[:, :, None, :], jnp.bfloat16(0))
            acc = acc + jnp.einsum("rect,ercd->td", wts, returned, preferred_element_type=jnp.float32)
        return acc.astype(jnp.bfloat16)

    return jax.shard_map(local_layer, mesh=mesh, in_specs=(row_spec, row_spec, row_spec, P("ep", None, "tp"), P("ep", None, "tp"), P("ep", "tp", None)), out_specs=row_spec, check_vma=False)
```

time: 2970 us -> 835 us (0.28)
  blocking collectives: 1670 us -> 15.2 us
  local copies, waits for them, and re-layouts: 208 us -> 28.3 us
  waiting for transfers between devices: 836 us -> 665 us
  other arithmetic: 72.2 us -> 1.44 us
  matrix products: 161 us -> 103 us
    all_to_all x2 -> x1, blocking collectives: 1670 us -> 15.2 us  [local_layer(): lax.all_to_all(slots.reshape(expert_ranks, local_exp, tok_loc), 'ep', 0,...]
    all_gather x1 -> x4, waiting for transfers between devices: 590 us -> 416 us  [the longest x1 123 us: local_layer(): wdt = lax.all_gather(wd_loc, 'tp')]
    broadcast_in_dim x4 -> x0, local copies, waits for them, and re-layouts: 112 us -> none  [the longest x1 112 us: local_layer(): pieces = lax.all_to_all(part_sums[None], 'tp', 2, 0, tiled=True)]
    reduce_sum x3 -> x1, other arithmetic: 61 us -> 0.35 us  [slot_map(): gates = jnp.sum(jnp.where(hit, gate_loc[None], 0.0), axis=2)]
    dot_general x3 -> x7, matrix products: 161 us -> 103 us  [the longest x1 38.5 us: local_layer(): jnp.einsum('ertf,tefd->erd', hidden, wdt, preferred_element_type=jnp.floa...]
    gather x2 -> x0, local copies, waits for them, and re-layouts: 57.1 us -> none  [the longest x1 32.7 us: local_layer(): jnp.take(x_loc, src_rows, axis=0)]
  transfers between devices with their start and end apart: 2 -> 5, of which waited for: 2 -> 5; matrix products, arithmetic and copies ran while one was open for 0% -> 6% of each run, Pallas kernels for 0% -> 0%
where the time goes in v1:
time: 835 us; the launch traced here: 834 us
  waiting for transfers between devices  665 us (80%)
  matrix products  103 us (12%)
  local copies, waits for them, and re-layouts  28.3 us (3%)
  blocking collectives  15.2 us (2%)
  between operations  13.2 us (2%)
    all_to_all x1, waiting for transfers between devices, local_layer(): returned = lax.all_to_all(y_rows, 'ep', 1, 1, tiled=True)  247 us
    all_gather x1, waiting for transfers between devices, local_layer(): wdt = lax.all_gather(wd_loc, 'tp')  123 us
    all_gather x1, waiting for transfers between devices, local_layer(): wgt = lax.all_gather(jnp.swapaxes(wg_loc, 1, 2), 'tp')  100 us
    all_gather x1, waiting for transfers between devices, local_layer(): tok_all = lax.all_gather(x_loc, 'ep')  97.6 us
    all_gather x1, waiting for transfers between devices, local_layer(): wut = lax.all_gather(jnp.swapaxes(wu_loc, 1, 2), 'tp')  94.8 us
    dot_general x1, matrix products, local_layer(): jnp.einsum('ertf,tefd->erd', hidden, wdt, preferred_element_type=jnp.floa...  38.5 us
    dot_general x3, matrix products, local_layer(): jnp.einsum('rect,ercd->td', wts, returned, preferred_element_type=jnp.flo...  27.6 us
    dot_general x1, matrix products, local_layer(): jnp.einsum('erd,tefd->ertf', rows, wut, preferred_element_type=jnp.float32)  23.1 us
  transfers between devices with their start and end apart: 5, of which 5 were waited for; matrix products, arithmetic and copies ran while one was open for 6% of the time, Pallas kernels for 0%

profile of v1, /device:TPU:1, one launch (start us, length us, event | category | flops | bytes accessed | tf_op | source)
XLA Modules:
  0.0 833.8 jit_solution(13819781300836326354)
XLA Ops:
  6.5 0.7 all-gather.9.cloned.1.call-update
  7.3 0.0 all-gather.13.cloned.1.call-start
  7.3 0.7 all-gather.13.cloned.1.call-update
  8.1 0.7 all-gather.11.cloned.1.call-update
  8.7 0.0 all-gather.15.cloned.1.call-start
  8.8 0.5 all-gather.15.cloned.1.call-update
  9.3 1.1 fusion.53
  10.4 0.2 select_bitcast_fusion
  10.6 15.2 %all_to_all.10 = f32[16,8,256]{2,1,0:T(8,128)S(1)} all-to-all(f32[16,8,256]{2,1,0:T(8,128)S(1)} %select_bitcast_fusion), channel_id=1, replica_groups=mesh['dp'=1,'ep'=16,'tp'=8] {'ep'}, dimensions={0} | all-to-all | bytes 262144 | tf_op jit(solution)/shard_map/all_to_all | solution.py:42
  25.8 97.6 %all-gather.9.cloned.1.call-done = bf16[4096,2048]{1,0:T(8,128)(2,1)} async-done(((bf16[256,2048]{1,0:T(8,128)(2,1)}), bf16[4096,2048]{1,0:T(8,128)(2,1)}) %all-gather.9.cloned.1.call-update) | async-done | bytes 16777232 | tf_op jit(solution)/shard_map/all_gather | solution.py:41
  123.4 13.8 %convert_bitcast_fusion = bf16[8,16,32,2048]{3,2,0,1:T(8,128)(2,1)} fusion(bf16[16,256,2048,1]{2,1,3,0:T(8,128)(2,1)} %bitcast.55, f32[16,8,256]{2,1,0:T(8,128)S(1)} %all_to_all.10), kind=kOutput, calls=%fused_computation.7 | convolution fusion | flops 4304404480 | bytes 33685504 | tf_op jit(solution)/shard_map/sect,std->escd/dot_general | solution.py:45
  137.2 14.1 %copy.48 = bf16[8,16,32,2048]{3,2,1,0:T(8,128)(2,1)} copy(bf16[8,16,32,2048]{3,2,0,1:T(8,128)(2,1)} %convert_bitcast_fusion) | data formatting | bytes 33554432 | tf_op jit(solution)/shard_map/convert_element_type | solution.py:45
  151.4 94.8 %all-gather.13.cloned.1.call-done = bf16[64,96,2048]{2,1,0:T(8,128)(2,1)} async-done(((bf16[8,96,2048]{2,1,0:T(8,128)(2,1)}), bf16[64,96,2048]{2,1,0:T(8,128)(2,1)}) %all-gather.13.cloned.1.call-update) | async-done | bytes 25165840 | tf_op jit(solution)/shard_map/all_gather | solution.py:38
  246.1 23.1 %fusion.2 = f32[8,512,8,96]{1,3,2,0:T(8,128)} fusion(bf16[8,512,2048,1]{2,1,3,0:T(8,128)(2,1)} %bitcast.56, bf16[8,8,96,2048]{3,2,1,0:T(8,128)(2,1)} %bitcast.61), kind=kOutput, calls=%fused_computation.3 | convolution fusion | flops 12884901888 | bytes 54525952 | tf_op jit(solution)/shard_map/erd,tefd->ertf/dot_general | solution.py:48
  269.2 100.3 %all-gather.11.cloned.1.call-done = bf16[64,96,2048]{2,1,0:T(8,128)(2,1)} async-done(((bf16[8,96,2048]{2,1,0:T(8,128)(2,1)}), bf16[64,96,2048]{2,1,0:T(8,128)(2,1)}) %all-gather.11.cloned.1.call-update) | async-done | bytes 25165840 | tf_op jit(solution)/shard_map/all_gather | solution.py:37
  369.5 123.3 %all-gather.15.cloned.1.call-done = bf16[64,96,2048]{2,1,0:T(8,128)(2,1)} async-done(((bf16[8,96,2048]{2,1,0:T(8,128)(2,1)}), bf16[64,96,2048]{2,1,0:T(8,128)(2,1)}) %all-gather.15.cloned.1.call-update) | async-done | bytes 25165840 | tf_op jit(solution)/shard_map/all_gather | solution.py:39
  492.8 38.5 %bitcast_convert_fusion = bf16[8,512,2048]{2,1,0:T(8,128)(2,1)} fusion(bf16[8,8,96,2048]{3,2,1,0:T(8,128)(2,1)} %bitcast.63, f32[8,512,8,96]{1,3,2,0:T(8,128)} %fusion.2, bf16[8,512,2048,1]{2,1,3,0:T(8,128)(2,1)} %bitcast.57, bf16[8,8,96,2048]{3,2,1,0:T(8,128)(2,1)} %bitcast.62), kind=kOutput, calls=%fused_computation | convolution fusion | flops 25797066752 | bytes 96468992 | tf_op jit(solution)/shard_map/ertf,tefd->erd/dot_general | solution.py:50
  531.3 14.1 %copy.52 = bf16[8,16,32,2048]{3,2,0,1:T(8,128)(2,1)} copy(bf16[8,16,32,2048]{3,2,1,0:T(8,128)(2,1)} %bitcast.58) | data formatting | bytes 33554432 | tf_op jit(solution)/shard_map/reshape | solution.py:51
  545.4 6.9 all-to-all-start.1
  552.4 0.3 select_reduce_fusion
  552.8 246.9 %all-to-all-done.1 = bf16[8,16,32,2048]{3,2,0,1:T(8,128)(2,1)} async-done(((bf16[8,16,32,2048]{3,2,0,1:T(8,128)(2,1)}), bf16[8,16,32,2048]{3,2,0,1:T(8,128)(2,1)}, u32[]{:S(2)}, u32[]{:S(2)}) %all-to-all-start.1) | async-done | bytes 16777248 | tf_op jit(solution)/shard_map/all_to_all | solution.py:52
  799.7 8.1 fusion.22
  807.9 8.2 fusion.34
  816.0 11.3 %fusion.37 = bf16[256,2048]{1,0:T(8,128)(2,1)} fusion(f32[256,2048]{1,0:T(8,128)S(1)} %fusion.34, bf16[8,16,32,2048]{3,2,0,1:T(8,128)(2,1)} %all-to-all-done.1, f32[16,8,256]{2,0,1:T(8,128)S(1)} %copy.46, bf16[16,8,256]{2,0,1:T(8,128)(2,1)S(1)} %copy.56), kind=kOutput, calls=%fused_computation.26 | convolution fusion | flops 4298113024 | bytes 20119552 | tf_op jit(solution)/shard_map/rect,ercd->td/dot_general | solution.py:58
  (11 shorter events, 0.2 us)
Async XLA Ops:
  6.5 116.9 %all-gather.9.cloned.1.call-start = ((), (), s32[]{:S(2)}) async-start(), calls=%async_computation.2 | async-start | bytes 17825792 | tf_op jit(solution)/shard_map/all_gather | solution.py:41
  7.3 238.9 %all-gather.13.cloned.1.call-start = ((), (), s32[]{:S(2)}) async-start(), calls=%async_computation.4 | async-start | bytes 28311552 | tf_op jit(solution)/shard_map/all_gather | solution.py:38
  8.0 361.5 %all-gather.11.cloned.1.call-start = ((), (), s32[]{:S(2)}) async-start(), calls=%async_computation.3 | async-start | bytes 28311552 | tf_op jit(solution)/shard_map/all_gather | solution.py:37
  8.7 484.1 %all-gather.15.cloned.1.call-start = ((), (), s32[]{:S(2)}) async-start(), calls=%async_computation.5 | async-start | bytes 28311552 | tf_op jit(solution)/shard_map/all_gather | solution.py:39
  545.4 7.0 copy-start
  545.4 7.0 copy-start.1
  545.4 254.3 %all-to-all-start.1 = ((bf16[8,16,32,2048]{3,2,0,1:T(8,128)(2,1)}), bf16[8,16,32,2048]{3,2,0,1:T(8,128)(2,1)}, u32[]{:S(2)}, u32[]{:S(2)}) async-start(bf16[8,16,32,2048]{3,2,0,1:T(8,128)(2,1)} %copy.52), calls=%async_computation.1 | async-start | bytes 33554432 | tf_op jit(solution)/shard_map/all_to_all | solution.py:52
Sparse Core Ops, SparseCore 0:
  9.5 113.9 all-gather.8
  125.1 120.9 all-gather.12
  247.8 121.6 all-gather.10
  371.1 121.6 all-gather.14

commit v2 on v1

v2 whole, which is shorter than its diff:
```python
import functools

import jax
import jax.numpy as jnp
from jax import lax
from jax.experimental import pallas as pl
from jax.experimental.pallas import tpu as pltpu
from jax.sharding import PartitionSpec as P

CAP_FACTOR = 2
RING = 4
CORES = 2
MESH = pl.DeviceIdType.MESH
F32 = jnp.float32
BF16 = jnp.bfloat16


def slot_map(ids_loc, gate_loc, n_exp, capacity):
    tok_loc = ids_loc.shape[0]
    hit = ids_loc[None, :, :] == jnp.arange(n_exp, dtype=jnp.int32)[:, None, None]
    chosen = jnp.any(hit, axis=2)
    gates = jnp.sum(jnp.where(hit, gate_loc[None], 0.0), axis=2)
    before = (jnp.arange(tok_loc)[:, None] < jnp.arange(tok_loc)[None, :]).astype(BF16)
    slots = jnp.dot(chosen.astype(BF16), before, preferred_element_type=F32)
    slots = jnp.where(chosen & (slots < capacity), slots, -1.0)
    return slots, gates


def remote(src, dst, send, recv, **device):
    return pltpu.make_async_remote_copy(src_ref=src, dst_ref=dst, send_sem=send, recv_sem=recv, device_id=device, device_id_type=MESH)


def moe_kernel(n_rank, n_loc, capacity, x_hbm, wg, wu, wd, slots_send, slots_own, gates_own, out, wfull, yret, tok, meta, rows_in, wbuf, ybuf, retbuf, acc, ring_s, ring_r, part_s, part_r, line_s, line_r, plane_s, plane_r, meta_s, meta_r, y_s, y_r, load_sem, own_sem, ret_sem, tok_sem):
    ep = lax.axis_index("ep")
    tp = lax.axis_index("tp")
    z, y = ep // RING, lax.rem(ep, RING)
    x, core = tp // CORES, lax.rem(tp, CORES)
    weights = (wg, wu, wd)
    cols = wg.shape[1]
    half = cols // 2
    tok_loc = x_hbm.shape[0]
    quart = tok_loc // 4
    n_rows = n_rank * capacity

    def step(pos, amount):
        return lax.rem(pos + amount + 2 * RING, RING)

    ring_to = (step(x, 1) * CORES + core, step(x, -1) * CORES + core)
    partner = x * CORES + 1 - core

    def chunk_rows(t, d):
        return pl.ds(pl.multiple_of(t * cols + d * half, 16), half)

    def ring_in_x(d, s):
        return step(x, -1 - s) if d == 0 else step(x, 1 + s)

    def ring_start(d, s, e):
        if s == 0:
            rows = chunk_rows(tp, d)
            for i, w in enumerate(weights):
                remote(w.at[e, pl.ds(d * half, half), :], wfull.at[e, i, rows, :], ring_s.at[d, s, e], ring_r.at[d, s, e], tp=ring_to[d]).start()
        else:
            piece = wfull.at[e, :, chunk_rows(ring_in_x(d, s - 1) * CORES + core, d), :]
            remote(piece, piece, ring_s.at[d, s, e], ring_r.at[d, s, e], tp=ring_to[d]).start()

    def ring_desc(d, s, e):
        piece = wfull.at[e, :, chunk_rows(ring_in_x(d, s) * CORES + core, d), :]
        return remote(piece, piece, ring_s.at[d, s, e], ring_r.at[d, s, e], tp=ring_to[d])

    def own_rows(t):
        return pl.ds(pl.multiple_of(t * cols, 16), cols)

    def share_own(e):
        for i, w in enumerate(weights):
            remote(w.at[e], wfull.at[e, i, own_rows(tp), :], part_s.at[6, e], part_r.at[6, e], tp=partner).start()

    def share_own_desc(e):
        piece = wfull.at[e, :, own_rows(partner), :]
        return remote(piece, piece, part_s.at[6, e], part_r.at[6, e], tp=partner)

    def share(d, s, e):
        piece = wfull.at[e, :, chunk_rows(ring_in_x(d, s) * CORES + core, d), :]
        remote(piece, piece, part_s.at[d * 3 + s, e], part_r.at[d * 3 + s, e], tp=partner).start()

    def share_desc(d, s, e):
        piece = wfull.at[e, :, chunk_rows(ring_in_x(d, s) * CORES + 1 - core, d), :]
        return remote(piece, piece, part_s.at[d * 3 + s, e], part_r.at[d * 3 + s, e], tp=partner)

    routes = (("y", 1), ("y", -1), ("z", 1), ("z", -1))

    def plane_peer(axis, amount):
        return z * RING + step(y, amount) if axis == "y" else step(z, amount) * RING + y

    def quarter(q):
        return pl.ds(q * quart, quart)

    def line_piece(q, back):
        axis, sign = routes[q]
        if axis == "y":
            return tok.at[z, step(y, -sign * back), quarter(q), :]
        return tok.at[step(z, -sign * back), y, quarter(q), :]

    def line_start(q, s):
        axis, sign = routes[q]
        src = x_hbm.at[quarter(q), :] if s == 0 else line_piece(q, s)
        remote(src, line_piece(q, s), line_s.at[q, s], line_r.at[q, s], ep=plane_peer(axis, sign)).start()

    def line_desc(q, s):
        axis, sign = routes[q]
        piece = line_piece(q, s + 1)
        return remote(piece, piece, line_s.at[q, s], line_r.at[q, s], ep=plane_peer(axis, sign))

    def plane_piece(q, back):
        axis, sign = routes[q]
        if axis == "y":
            return tok.at[step(z, -sign * back), :, quarter(q), :]
        return tok.at[:, step(y, -sign * back), quarter(q), :]

    def plane_start(q, s):
        axis, sign = routes[q]
        piece = plane_piece(q, s)
        remote(piece, piece, plane_s.at[q, s], plane_r.at[q, s], ep=plane_peer("z" if axis == "y" else "y", sign)).start()

    def plane_desc(q, s):
        axis, sign = routes[q]
        piece = plane_piece(q, s + 1)
        return remote(piece, piece, plane_s.at[q, s], plane_r.at[q, s], ep=plane_peer("z" if axis == "y" else "y", sign))

    def peer(j):
        return lax.rem(ep + j, n_rank)

    def back_peer(j):
        return lax.rem(ep + n_rank - j, n_rank)

    def src_rows(r):
        return pl.ds(pl.multiple_of(r * capacity, capacity), capacity)

    def y_send(e, k, j):
        r = peer(j)
        return remote(ybuf.at[k, src_rows(r), :], yret.at[e, ep], y_s.at[k, j], y_r.at[e, j], ep=r)

    def y_recv(e, j):
        r = back_peer(j)
        return remote(yret.at[e, r], yret.at[e, r], y_s.at[0, j], y_r.at[e, j], ep=peer(j))

    def y_own(e, k):
        return pltpu.make_async_copy(ybuf.at[k, src_rows(ep), :], yret.at[e, ep], own_sem.at[k])

    barrier = pltpu.get_barrier_semaphore()
    for j in range(1, n_rank):
        pl.semaphore_signal(barrier, inc=1, device_id={"ep": peer(j)}, device_id_type=MESH)
    for t in (*ring_to, partner):
        pl.semaphore_signal(barrier, inc=1, device_id={"tp": t}, device_id_type=MESH)
    pl.semaphore_wait(barrier, n_rank - 1 + 3)

    def ring_issue(b, static):
        def when(cond, fn):
            if static:
                if cond:
                    fn()
            else:
                pl.when(cond)(fn)

        def first():
            for d in range(2):
                ring_desc(d, 0, b).wait_recv()
                ring_start(d, 1, b)
            for d in range(2):
                share(d, 0, b)

        def second():
            for d in range(2):
                ring_desc(d, 1, b - 1).wait_recv()
                ring_start(d, 2, b - 1)
            for d in range(2):
                share(d, 1, b - 1)

        def ahead():
            for d in range(2):
                ring_start(d, 0, b + 2)
            share_own(b + 2)

        when(b < n_loc, first)
        if static:
            if 1 <= b:
                second()
        else:
            pl.when(b <= n_loc)(second)
        when(b + 2 < n_loc, ahead)

    def combine(e):
        for j in range(1, n_rank):
            y_recv(e, j).wait_recv()
        y_own(e, lax.rem(e, 2)).wait()
        load = pltpu.make_async_copy(yret.at[e], retbuf, ret_sem)
        load.start()
        slot_iota = lax.broadcasted_iota(jnp.int32, (n_rank, capacity, tok_loc), 1).astype(F32)
        place = slots_own[e][:, None, :] == slot_iota
        mix = jnp.where(place, gates_own[e][:, None, :], 0.0).reshape(n_rows, tok_loc).T
        hi = mix.astype(BF16)
        rest = mix - hi.astype(F32)
        mid = rest.astype(BF16)
        low = (rest - mid.astype(F32)).astype(BF16)
        load.wait()
        for n in range(4):
            width = acc.shape[1] // 4
            blk = pl.ds(n * width, width)
            ret = retbuf[:, :, blk].reshape(n_rows, width)
            acc[:, blk] += jnp.dot(hi, ret, preferred_element_type=F32) + jnp.dot(mid, ret, preferred_element_type=F32) + jnp.dot(low, ret, preferred_element_type=F32)

    def expert(e, static_first=False):
        for d in range(2):
            ring_desc(d, 2, e).wait_recv()
            share(d, 2, e)
        share_own_desc(e).wait_recv()
        for d in range(2):
            for s in range(3):
                share_desc(d, s, e).wait_recv()
        copies = []
        for i, w in enumerate(weights):
            copies.append(pltpu.make_async_copy(w.at[e], wbuf.at[i, own_rows(tp), :], load_sem.at[i]))
        for j in range(1, RING * CORES):
            other = own_rows(lax.rem(tp + j, RING * CORES))
            copies.append(pltpu.make_async_copy(wfull.at[e, :, other, :], wbuf.at[:, other, :], load_sem.at[2 + j]))
        for c in copies:
            c.start()
        k = lax.rem(e, 2)

        @pl.when(e >= 2)
        def _():
            for j in range(1, n_rank):
                y_send(e - 2, k, j).wait_send()

        for c in copies:
            c.wait()
        xe = rows_in[e]
        hidden = []
        for f in range(3):
            blk = pl.ds(f * 256, 256)
            dims = (((1,), (1,)), ((), ()))
            a = lax.dot_general(xe, wbuf[0, blk, :], dims, preferred_element_type=F32)
            b = lax.dot_general(xe, wbuf[1, blk, :], dims, preferred_element_type=F32)
            hidden.append((jax.nn.silu(a) * b).astype(BF16))
        h = jnp.concatenate(hidden, axis=1)
        for n in range(4):
            width = ybuf.shape[2] // 4
            blk = pl.ds(n * width, width)
            ybuf[k, :, blk] = jnp.dot(h, wbuf[2, :, blk], preferred_element_type=F32).astype(BF16)
        y_own(e, k).start()
        for j in range(1, n_rank):
            y_send(e, k, j).start()

    for b in range(2):
        for d in range(2):
            ring_start(d, 0, b)
    for q in range(4):
        line_start(q, 0)
    load_own = pltpu.make_async_copy(x_hbm, tok.at[z, y], tok_sem)
    load_own.start()
    for j in range(1, n_rank):
        remote(slots_send.at[peer(j)], meta.at[ep], meta_s.at[j], meta_r.at[j], ep=peer(j)).start()
    for b in range(2):
        share_own(b)
    meta[ep] = slots_send[ep]
    acc[...] = jnp.zeros_like(acc)
    for s in range(2):
        for q in range(4):
            line_desc(q, s).wait_recv()
            line_start(q, s + 1)
    ring_issue(0, True)
    load_own.wait()
    for q in range(4):
        line_desc(q, 2).wait_recv()
    for q in range(4):
        plane_start(q, 0)
    ring_issue(1, True)
    for q in range(4):
        plane_desc(q, 0).wait_recv()
        plane_start(q, 1)
    ring_issue(2, True)
    for q in range(4):
        plane_desc(q, 1).wait_recv()
        plane_start(q, 2)
    for q in range(4):
        plane_desc(q, 2).wait_recv()
    for j in range(1, n_rank):
        remote(slots_send.at[back_peer(j)], meta.at[back_peer(j)], meta_s.at[j], meta_r.at[j], ep=peer(j)).wait_recv()

    @pl.loop(0, n_rank)
    def _(s):
        slot_iota = lax.broadcasted_iota(jnp.int32, (n_loc, capacity, tok_loc), 1).astype(F32)
        pick = jnp.where(meta[s][:, None, :] == slot_iota, 1.0, 0.0).reshape(n_loc * capacity, tok_loc).astype(BF16)
        picked = jnp.dot(pick, tok[s // RING, lax.rem(s, RING)], preferred_element_type=F32).astype(BF16)
        for e in range(n_loc):
            rows_in[e, src_rows(s), :] = picked[e * capacity:(e + 1) * capacity]

    @pl.loop(2, n_loc + 2)
    def _(b):
        @pl.when(b > 2)
        def _():
            ring_issue(b, False)

        expert(b - 2)

        @pl.when(b > 2)
        def _():
            combine(b - 3)

    combine(n_loc - 1)
    out[...] = acc[...].astype(out.dtype)

    for e in (n_loc - 2, n_loc - 1):
        k = e % 2
        for j in range(1, n_rank):
            y_send(e, k, j).wait_send()
    for q in range(4):
        for s in range(3):
            line_desc(q, s).wait_send()
            plane_desc(q, s).wait_send()
    for j in range(1, n_rank):
        remote(slots_send.at[peer(j)], meta.at[ep], meta_s.at[j], meta_r.at[j], ep=peer(j)).wait_send()

    @pl.loop(0, n_loc)
    def _(e):
        share_own_desc(e).wait_send()
        for d in range(2):
            for s in range(3):
                ring_desc(d, s, e).wait_send()
                share_desc(d, s, e).wait_send()


def solution(mesh):
    expert_ranks = mesh.shape["ep"]
    row_spec = P(("dp", "ep", "tp"), None)

    def local_layer(x_loc, ids_loc, gate_loc, wg_loc, wu_loc, wd_loc):
        tok_loc, d_model = x_loc.shape
        n_top = ids_loc.shape[1]
        local_exp, _, cols = wg_loc.shape
        ffn = cols * mesh.shape["tp"]
        n_exp = local_exp * expert_ranks
        capacity = CAP_FACTOR * n_top * tok_loc // n_exp
        n_rows = expert_ranks * capacity
        slots, gates = slot_map(ids_loc, gate_loc, n_exp, capacity)
        slots = slots.reshape(expert_ranks, local_exp, tok_loc)
        gates = gates.reshape(expert_ranks, local_exp, tok_loc)
        any_spec = pl.BlockSpec(memory_space=pl.ANY)
        vmem_spec = pl.BlockSpec(memory_space=pltpu.VMEM)
        dma = pltpu.SemaphoreType.DMA
        out = pl.pallas_call(
            functools.partial(moe_kernel, expert_ranks, local_exp, capacity),
            out_shape=(
                jax.ShapeDtypeStruct((tok_loc, d_model), BF16),
                jax.ShapeDtypeStruct((local_exp, 3, ffn, d_model), BF16),
                jax.ShapeDtypeStruct((local_exp, expert_ranks, capacity, d_model), BF16),
            ),
            in_specs=[any_spec] * 4 + [vmem_spec] * 3,
            out_specs=(vmem_spec, any_spec, any_spec),
            scratch_shapes=[
                pltpu.VMEM((RING, RING, tok_loc, d_model), BF16),
                pltpu.VMEM((expert_ranks, local_exp, tok_loc), F32),
                pltpu.VMEM((local_exp, n_rows, d_model), BF16),
                pltpu.VMEM((3, ffn, d_model), BF16),
                pltpu.VMEM((2, n_rows, d_model), BF16),
                pltpu.VMEM((expert_ranks, capacity, d_model), BF16),
                pltpu.VMEM((tok_loc, d_model), F32),
                dma((2, 3, local_exp)),
                dma((2, 3, local_exp)),
                dma((7, local_exp)),
                dma((7, local_exp)),
                dma((4, 3)),
                dma((4, 3)),
                dma((4, 3)),
                dma((4, 3)),
                dma((expert_ranks,)),
                dma((expert_ranks,)),
                dma((2, expert_ranks)),
                dma((local_exp, expert_ranks)),
                dma((10,)),
                dma((2,)),
                dma,
                dma,
            ],
            compiler_params=pltpu.CompilerParams(collective_id=0, has_side_effects=True, vmem_limit_bytes=67000000),
        )(
            x_loc,
            jnp.swapaxes(wg_loc, 1, 2),
            jnp.swapaxes(wu_loc, 1, 2),
            wd_loc,
            slots,
            jnp.swapaxes(slots, 0, 1),
            jnp.swapaxes(gates, 0, 1),
        )
        return out[0]

    return jax.shard_map(local_layer, mesh=mesh, in_specs=(row_spec, row_spec, row_spec, P("ep", None, "tp"), P("ep", None, "tp"), P("ep", "tp", None)), out_specs=row_spec, check_vma=False)
```

time: 835 us -> 387 us (0.46)
  waiting for transfers between devices: 665 us -> 0 us
  Pallas kernels: 0 us -> 380 us
  matrix products: 103 us -> 0.18 us
  local copies, waits for them, and re-layouts: 28.3 us -> 3.09 us
  blocking collectives: 15.2 us -> 0 us
  between operations: 13.2 us -> 0.03 us
    all_gather x4 -> x0, waiting for transfers between devices: 416 us -> none  [the longest x1 123 us: local_layer(): wdt = lax.all_gather(wd_loc, 'tp')]
    pallas_call x0 -> x1, Pallas kernels: none -> 380 us  [local_layer(): pl.pallas_call(functools.partial(moe_kernel, expert_ranks, local_exp, cap...]
    all_to_all x1 -> x0, waiting for transfers between devices: 247 us -> none  [local_layer(): returned = lax.all_to_all(y_rows, 'ep', 1, 1, tiled=True)]
    dot_general x7 -> x1, matrix products: 103 us -> 0.18 us  [slot_map(): slots = jnp.dot(chosen.astype(BF16), before, preferred_element_type=F32)]
    all_to_all x1 -> x0, blocking collectives: 15.2 us -> none  [local_layer(): lax.all_to_all(slots.reshape(expert_ranks, local_exp, tok_loc), 'ep', 0,...]
    convert_element_type x4 -> x0, local copies, waits for them, and re-layouts: 14.2 us -> none  [the longest x1 14.1 us: local_layer(): jnp.einsum('sect,std->escd', pick, tok_all, preferred_element_type=jnp.fl...]
    reshape x1 -> x0, local copies, waits for them, and re-layouts: 14.1 us -> none  [local_layer(): y_rows = y_rows.reshape(local_exp, expert_ranks, capacity, d_model)]
  transfers between devices with their start and end apart: 5 -> 0, of which waited for: 5 -> 0; matrix products, arithmetic and copies ran while one was open for 6% -> 0% of each run, Pallas kernels for 0% -> 0%
where the time goes in v2:
time: 387 us; the launch traced here: 386 us
  Pallas kernels  380 us (98%)
    pallas_call x1, Pallas kernels, local_layer(): pl.pallas_call(functools.partial(moe_kernel, expert_ranks, local_exp, cap...  380 us

profile of v2, /device:TPU:1, one launch (start us, length us, event | category | flops | bytes accessed | tf_op | source)
XLA Modules:
  0.0 386.0 jit_solution(15695171604458811216)
XLA Ops:
  0.0 1.1 fusion
  1.1 0.2 select_bitcast_fusion.slots_send
  1.2 0.0 copy-start
  1.3 1.1 select_reduce_fusion
  2.4 0.0 copy-done
  2.4 0.8 copy_bitcast_fusion
  3.2 380.5 %shard_map.64 = (bf16[256,2048]{1,0:T(8,128)(2,1)}, bf16[8,3,768,2048]{3,2,1,0:T(8,128)(2,1)}, bf16[8,16,32,2048]{3,2,1,0:T(8,128)(2,1)}) custom-call(bf16[256,2048]{1,0:T(8,128)(2,1)} %x_hbm.1, bf16[8,96,2048]{2,1,0:T(8,128)(2,1)} %bitcast.10, bf16[8,96,2048]{2,1,0:T(8,128)(2,1)} %bitcast.11, bf16[8,96,2048]{2,1,0:T(8,128)(2,1)} %wd.1, ...), custom_call_target="tpu_custom_call" | custom-call | tf_op jit(solution)/shard_map/pallas_call | solution.py:350
  383.7 2.3 copy.19
Async XLA Ops:
  1.2 1.1 copy-start

commit v3 on v2

--- a/solution.py
+++ b/solution.py
@@ -15,22 +15,15 @@
 BF16 = jnp.bfloat16
 
 
-def slot_map(ids_loc, gate_loc, n_exp, capacity):
-    tok_loc = ids_loc.shape[0]
-    hit = ids_loc[None, :, :] == jnp.arange(n_exp, dtype=jnp.int32)[:, None, None]
-    chosen = jnp.any(hit, axis=2)
-    gates = jnp.sum(jnp.where(hit, gate_loc[None], 0.0), axis=2)
-    before = (jnp.arange(tok_loc)[:, None] < jnp.arange(tok_loc)[None, :]).astype(BF16)
-    slots = jnp.dot(chosen.astype(BF16), before, preferred_element_type=F32)
-    slots = jnp.where(chosen & (slots < capacity), slots, -1.0)
-    return slots, gates
+ROUND = ((0, 1), (0, -1), (1, 0), (-1, 0), (2, 2), (1, 1), (-1, -1), (1, -1), (-1, 1), (0, 2), (2, 0), (2, 1), (1, 2), (2, -1), (-1, 2))
+BLOCKS = 4
 
 
 def remote(src, dst, send, recv, **device):
     return pltpu.make_async_remote_copy(src_ref=src, dst_ref=dst, send_sem=send, recv_sem=recv, device_id=device, device_id_type=MESH)
 
 
-def moe_kernel(n_rank, n_loc, capacity, x_hbm, wg, wu, wd, slots_send, slots_own, gates_own, out, wfull, yret, tok, meta, rows_in, wbuf, ybuf, retbuf, acc, ring_s, ring_r, part_s, part_r, line_s, line_r, plane_s, plane_r, meta_s, meta_r, y_s, y_r, load_sem, own_sem, ret_sem, tok_sem):
+def moe_kernel(n_rank, n_loc, capacity, x_hbm, wg, wu, wd, ids, gate_vals, out, wfull, yret, tok, meta, slots_send, slots_own, gates_own, rows_in, wbuf, ybuf, retbuf, acc, ring_s, ring_r, part_s, part_r, fine_s, fine_r, fpart_s, fpart_r, line_s, line_r, plane_s, plane_r, meta_s, meta_r, y_s, y_r, yb_s, yb_r, load_sem, own_sem, ownb_sem, ret_sem, retb_sem, tok_sem):
     ep = lax.axis_index("ep")
     tp = lax.axis_index("tp")
     z, y = ep // RING, lax.rem(ep, RING)
@@ -86,6 +79,81 @@
         piece = wfull.at[e, :, chunk_rows(ring_in_x(d, s) * CORES + 1 - core, d), :]
         return remote(piece, piece, part_s.at[d * 3 + s, e], part_r.at[d * 3 + s, e], tp=partner)
 
+    coarse = n_loc - 2
+    width = x_hbm.shape[1] // BLOCKS
+    parts6 = (0, 1, 2)
+    parts7 = (3, 4)
+    down7 = tuple(range(5, 5 + BLOCKS))
+
+    def fine_at(q):
+        if q < 3:
+            return coarse, q, slice(None)
+        if q < 5:
+            return coarse + 1, q - 3, slice(None)
+        return coarse + 1, 2, pl.ds((q - 5) * width, width)
+
+    def fine_own(q, rows):
+        e, i, c = fine_at(q)
+        return weights[i].at[e, rows, c]
+
+    def fine_land(q, rows):
+        e, i, c = fine_at(q)
+        return wfull.at[e, i, rows, c]
+
+    def fine_start(d, s, q):
+        if s == 0:
+            src, dst = fine_own(q, pl.ds(d * half, half)), fine_land(q, chunk_rows(tp, d))
+        else:
+            src = dst = fine_land(q, chunk_rows(ring_in_x(d, s - 1) * CORES + core, d))
+        remote(src, dst, fine_s.at[d, s, q], fine_r.at[d, s, q], tp=ring_to[d]).start()
+
+    def fine_desc(d, s, q):
+        piece = fine_land(q, chunk_rows(ring_in_x(d, s) * CORES + core, d))
+        return remote(piece, piece, fine_s.at[d, s, q], fine_r.at[d, s, q], tp=ring_to[d])
+
+    def fine_share_own(q):
+        remote(fine_own(q, pl.ds(0, cols)), fine_land(q, own_rows(tp)), fpart_s.at[6, q], fpart_r.at[6, q], tp=partner).start()
+
+    def fine_share_own_desc(q):
+        piece = fine_land(q, own_rows(partner))
+        return remote(piece, piece, fpart_s.at[6, q], fpart_r.at[6, q], tp=partner)
+
+    def fine_share(d, s, q):
+        piece = fine_land(q, chunk_rows(ring_in_x(d, s) * CORES + core, d))
+        remote(piece, piece, fpart_s.at[d * 3 + s, q], fpart_r.at[d * 3 + s, q], tp=partner).start()
+
+    def fine_share_desc(d, s, q):
+        piece = fine_land(q, chunk_rows(ring_in_x(d, s) * CORES + 1 - core, d))
+        return remote(piece, piece, fpart_s.at[d * 3 + s, q], fpart_r.at[d * 3 + s, q], tp=partner)
+
+    def fine_forward(s, items):
+        for q in items:
+            for d in range(2):
+                fine_desc(d, s, q).wait_recv()
+                if s < 2:
+                    fine_start(d, s + 1, q)
+                else:
+                    fine_share(d, s, q)
+
+    def fine_share_all(s, items):
+        for q in items:
+            for d in range(2):
+                fine_share(d, s, q)
+
+    def fine_load(q):
+        fine_share_own_desc(q).wait_recv()
+        for d in range(2):
+            for s in range(3):
+                fine_share_desc(d, s, q).wait_recv()
+        e, i, c = fine_at(q)
+        copies = [pltpu.make_async_copy(fine_own(q, pl.ds(0, cols)), wbuf.at[i, own_rows(tp), c], load_sem.at[q, 0])]
+        for j in range(1, RING * CORES):
+            other = own_rows(lax.rem(tp + j, RING * CORES))
+            copies.append(pltpu.make_async_copy(fine_land(q, other), wbuf.at[i, other, c], load_sem.at[q, j]))
+        for c in copies:
+            c.start()
+        return copies
+
     routes = (("y", 1), ("y", -1), ("z", 1), ("z", -1))
 
     def plane_peer(axis, amount):
@@ -127,10 +195,12 @@
         return remote(piece, piece, plane_s.at[q, s], plane_r.at[q, s], ep=plane_peer("z" if axis == "y" else "y", sign))
 
     def peer(j):
-        return lax.rem(ep + j, n_rank)
+        dz, dy = ROUND[j - 1]
+        return step(z, dz) * RING + step(y, dy)
 
     def back_peer(j):
-        return lax.rem(ep + n_rank - j, n_rank)
+        dz, dy = ROUND[j - 1]
+        return step(z, -dz) * RING + step(y, -dy)
 
     def src_rows(r):
         return pl.ds(pl.multiple_of(r * capacity, capacity), capacity)
@@ -145,6 +215,19 @@
 
     def y_own(e, k):
         return pltpu.make_async_copy(ybuf.at[k, src_rows(ep), :], yret.at[e, ep], own_sem.at[k])
+
+    def yb_send(n, j):
+        r, c = peer(j), pl.ds(n * width, width)
+        return remote(ybuf.at[1, src_rows(r), c], yret.at[n_loc - 1, ep, :, c], yb_s.at[n, j], yb_r.at[n, j], ep=r)
+
+    def yb_recv(n, j):
+        r, c = back_peer(j), pl.ds(n * width, width)
+        piece = yret.at[n_loc - 1, r, :, c]
+        return remote(piece, piece, yb_s.at[n, j], yb_r.at[n, j], ep=peer(j))
+
+    def yb_own(n):
+        c = pl.ds(n * width, width)
+        return pltpu.make_async_copy(ybuf.at[1, src_rows(ep), c], yret.at[n_loc - 1, ep, :, c], ownb_sem.at[n])
 
     barrier = pltpu.get_barrier_semaphore()
     for j in range(1, n_rank):
@@ -180,20 +263,23 @@
                 ring_start(d, 0, b + 2)
             share_own(b + 2)
 
-        when(b < n_loc, first)
+        def ahead_fine():
+            for q in parts6:
+                for d in range(2):
+                    fine_start(d, 0, q)
+            for q in parts6:
+                fine_share_own(q)
+
+        first()
         if static:
             if 1 <= b:
                 second()
         else:
-            pl.when(b <= n_loc)(second)
-        when(b + 2 < n_loc, ahead)
-
-    def combine(e):
-        for j in range(1, n_rank):
-            y_recv(e, j).wait_recv()
-        y_own(e, lax.rem(e, 2)).wait()
-        load = pltpu.make_async_copy(yret.at[e], retbuf, ret_sem)
-        load.start()
+            second()
+        when(b + 2 < coarse, ahead)
+        when(b + 2 == coarse, ahead_fine)
+
+    def mix_parts(e):
         slot_iota = lax.broadcasted_iota(jnp.int32, (n_rank, capacity, tok_loc), 1).astype(F32)
         place = slots_own[e][:, None, :] == slot_iota
         mix = jnp.where(place, gates_own[e][:, None, :], 0.0).reshape(n_rows, tok_loc).T
@@ -201,14 +287,41 @@
         rest = mix - hi.astype(F32)
         mid = rest.astype(BF16)
         low = (rest - mid.astype(F32)).astype(BF16)
+        return hi, mid, low
+
+    def mixed(parts, ret):
+        ret = ret.reshape(n_rows, width)
+        hi, mid, low = (jnp.dot(p, ret, preferred_element_type=F32) for p in parts)
+        return hi + mid + low
+
+    def combine(e):
+        for j in range(1, n_rank):
+            y_recv(e, j).wait_recv()
+        y_own(e, e % 2 if isinstance(e, int) else lax.rem(e, 2)).wait()
+        load = pltpu.make_async_copy(yret.at[e], retbuf, ret_sem)
+        load.start()
+        parts = mix_parts(e)
         load.wait()
-        for n in range(4):
-            width = acc.shape[1] // 4
+        for n in range(BLOCKS):
             blk = pl.ds(n * width, width)
-            ret = retbuf[:, :, blk].reshape(n_rows, width)
-            acc[:, blk] += jnp.dot(hi, ret, preferred_element_type=F32) + jnp.dot(mid, ret, preferred_element_type=F32) + jnp.dot(low, ret, preferred_element_type=F32)
-
-    def expert(e, static_first=False):
+            acc[:, blk] += mixed(parts, retbuf[:, :, blk])
+
+    def hidden_of(e):
+        xe = rows_in[e]
+        hidden = []
+        for f in range(3):
+            blk = pl.ds(f * 256, 256)
+            dims = (((1,), (1,)), ((), ()))
+            a = lax.dot_general(xe, wbuf[0, blk, :], dims, preferred_element_type=F32)
+            b = lax.dot_general(xe, wbuf[1, blk, :], dims, preferred_element_type=F32)
+            hidden.append((jax.nn.silu(a) * b).astype(BF16))
+        return jnp.concatenate(hidden, axis=1)
+
+    def down(h, k, n):
+        blk = pl.ds(n * width, width)
+        ybuf[k, :, blk] = jnp.dot(h, wbuf[2, :, blk], preferred_element_type=F32).astype(BF16)
+
+    def expert(e):
         for d in range(2):
             ring_desc(d, 2, e).wait_recv()
             share(d, 2, e)
@@ -218,34 +331,28 @@
                 share_desc(d, s, e).wait_recv()
         copies = []
         for i, w in enumerate(weights):
-            copies.append(pltpu.make_async_copy(w.at[e], wbuf.at[i, own_rows(tp), :], load_sem.at[i]))
+            copies.append(pltpu.make_async_copy(w.at[e], wbuf.at[i, own_rows(tp), :], load_sem.at[0, i]))
         for j in range(1, RING * CORES):
             other = own_rows(lax.rem(tp + j, RING * CORES))
-            copies.append(pltpu.make_async_copy(wfull.at[e, :, other, :], wbuf.at[:, other, :], load_sem.at[2 + j]))
+            copies.append(pltpu.make_async_copy(wfull.at[e, :, other, :], wbuf.at[:, other, :], load_sem.at[1, j]))
         for c in copies:
             c.start()
-        k = lax.rem(e, 2)
-
-        @pl.when(e >= 2)
-        def _():
+        k = e % 2 if isinstance(e, int) else lax.rem(e, 2)
+
+        def free_slot():
             for j in range(1, n_rank):
                 y_send(e - 2, k, j).wait_send()
 
+        if isinstance(e, int):
+            free_slot()
+        else:
+            pl.when(e >= 2)(free_slot)
+
         for c in copies:
             c.wait()
-        xe = rows_in[e]
-        hidden = []
-        for f in range(3):
-            blk = pl.ds(f * 256, 256)
-            dims = (((1,), (1,)), ((), ()))
-            a = lax.dot_general(xe, wbuf[0, blk, :], dims, preferred_element_type=F32)
-            b = lax.dot_general(xe, wbuf[1, blk, :], dims, preferred_element_type=F32)
-            hidden.append((jax.nn.silu(a) * b).astype(BF16))
-        h = jnp.concatenate(hidden, axis=1)
-        for n in range(4):
-            width = ybuf.shape[2] // 4
-            blk = pl.ds(n * width, width)
-            ybuf[k, :, blk] = jnp.dot(h, wbuf[2, :, blk], preferred_element_type=F32).astype(BF16)
+        h = hidden_of(e)
+        for n in range(BLOCKS):
+            down(h, k, n)
         y_own(e, k).start()
         for j in range(1, n_rank):
             y_send(e, k, j).start()
@@ -257,16 +364,37 @@
         line_start(q, 0)
     load_own = pltpu.make_async_copy(x_hbm, tok.at[z, y], tok_sem)
     load_own.start()
-    for j in range(1, n_rank):
-        remote(slots_send.at[peer(j)], meta.at[ep], meta_s.at[j], meta_r.at[j], ep=peer(j)).start()
     for b in range(2):
         share_own(b)
-    meta[ep] = slots_send[ep]
+
+    n_exp = n_rank * n_loc
+    row = lax.broadcasted_iota(jnp.int32, (n_exp, tok_loc), 0)
+    square = (tok_loc, tok_loc)
+    before = jnp.where(lax.broadcasted_iota(jnp.int32, square, 0) < lax.broadcasted_iota(jnp.int32, square, 1), 1.0, 0.0).astype(BF16)
+
+    def slot_map(expert_of_row):
+        chosen = jnp.zeros((n_exp, tok_loc), F32)
+        gates = jnp.zeros((n_exp, tok_loc), F32)
+        for j in range(ids.shape[0]):
+            hit = ids[j:j + 1, :] == expert_of_row
+            chosen = jnp.where(hit, 1.0, chosen)
+            gates = jnp.where(hit, gate_vals[j:j + 1, :], gates)
+        slots = jnp.dot(chosen.astype(BF16), before, preferred_element_type=F32)
+        return jnp.where((chosen > 0.5) & (slots < capacity - 0.5), slots, -1.0), gates
+
+    slots_send[...] = slot_map(row)[0].reshape(slots_send.shape)
+    slots, gates = slot_map(lax.rem(row, n_rank) * n_loc + row // n_rank)
+    slots_own[...] = slots.reshape(slots_own.shape)
+    gates_own[...] = gates.reshape(gates_own.shape)
     acc[...] = jnp.zeros_like(acc)
     for s in range(2):
         for q in range(4):
             line_desc(q, s).wait_recv()
             line_start(q, s + 1)
+        if s == 0:
+            for j in range(1, n_rank):
+                remote(slots_send.at[peer(j)], meta.at[ep], meta_s.at[j], meta_r.at[j], ep=peer(j)).start()
+            meta[ep] = slots_send[ep]
     ring_issue(0, True)
     load_own.wait()
     for q in range(4):
@@ -294,7 +422,7 @@
         for e in range(n_loc):
             rows_in[e, src_rows(s), :] = picked[e * capacity:(e + 1) * capacity]
 
-    @pl.loop(2, n_loc + 2)
+    @pl.loop(2, coarse)
     def _(b):
         @pl.when(b > 2)
         def _():
@@ -306,13 +434,87 @@
         def _():
             combine(b - 3)
 
-    combine(n_loc - 1)
-    out[...] = acc[...].astype(out.dtype)
-
-    for e in (n_loc - 2, n_loc - 1):
-        k = e % 2
+    for d in range(2):
+        ring_desc(d, 1, coarse - 1).wait_recv()
+        ring_start(d, 2, coarse - 1)
+        share(d, 1, coarse - 1)
+    fine_forward(0, parts6)
+    fine_share_all(0, parts6)
+    expert(coarse - 2)
+    combine(coarse - 3)
+    expert(coarse - 1)
+    fine_forward(1, parts6)
+    for q in parts7 + down7:
+        for d in range(2):
+            fine_start(d, 0, q)
+    fine_share_all(1, parts6)
+    for q in parts7 + down7:
+        fine_share_own(q)
+    combine(coarse - 2)
+
+    fine_forward(2, parts6)
+    loads = fine_load(0) + fine_load(1)
+    for c in loads:
+        c.wait()
+    loads = fine_load(2)
+    h = hidden_of(coarse)
+    fine_forward(0, parts7)
+    fine_share_all(0, parts7)
+    for j in range(1, n_rank):
+        y_send(coarse - 2, 0, j).wait_send()
+    for c in loads:
+        c.wait()
+    for n in range(BLOCKS):
+        down(h, 0, n)
+    y_own(coarse, 0).start()
+    for j in range(1, n_rank):
+        y_send(coarse, 0, j).start()
+
+    fine_forward(1, parts7)
+    fine_forward(0, down7)
+    fine_share_all(1, parts7)
+    fine_share_all(0, down7)
+    combine(coarse - 1)
+    fine_forward(2, parts7)
+    fine_forward(1, down7)
+    fine_share_all(1, down7)
+    loads = fine_load(3) + fine_load(4)
+    for c in loads:
+        c.wait()
+    h = hidden_of(coarse + 1)
+    for j in range(1, n_rank):
+        y_send(coarse - 1, 1, j).wait_send()
+    fine_forward(2, down7)
+    block_loads = [fine_load(q) for q in down7]
+    for n in range(BLOCKS):
+        for c in block_loads[n]:
+            c.wait()
+        down(h, 1, n)
+        yb_own(n).start()
         for j in range(1, n_rank):
-            y_send(e, k, j).wait_send()
+            yb_send(n, j).start()
+    combine(coarse)
+    parts = mix_parts(coarse + 1)
+    for n in range(BLOCKS):
+        blk = pl.ds(n * width, width)
+        for j in range(1, n_rank):
+            yb_recv(n, j).wait_recv()
+        yb_own(n).wait()
+        load = pltpu.make_async_copy(yret.at[coarse + 1, :, :, blk], retbuf.at[:, :, blk], retb_sem.at[n])
+        load.start()
+        load.wait()
+        out[:, blk] = (acc[:, blk] + mixed(parts, retbuf[:, :, blk])).astype(out.dtype)
+
+    for j in range(1, n_rank):
+        y_send(coarse, 0, j).wait_send()
+        for n in range(BLOCKS):
+            yb_send(n, j).wait_send()
+    for q in range(5 + BLOCKS):
+        fine_share_own_desc(q).wait_send()
+        for d in range(2):
+            for s in range(3):
+                fine_desc(d, s, q).wait_send()
+                fine_share_desc(d, s, q).wait_send()
     for q in range(4):
         for s in range(3):
             line_desc(q, s).wait_send()
@@ -320,7 +522,7 @@
     for j in range(1, n_rank):
         remote(slots_send.at[peer(j)], meta.at[ep], meta_s.at[j], meta_r.at[j], ep=peer(j)).wait_send()
 
-    @pl.loop(0, n_loc)
+    @pl.loop(0, coarse)
     def _(e):
         share_own_desc(e).wait_send()
         for d in range(2):
@@ -341,9 +543,6 @@
         n_exp = local_exp * expert_ranks
         capacity = CAP_FACTOR * n_top * tok_loc // n_exp
         n_rows = expert_ranks * capacity
-        slots, gates = slot_map(ids_loc, gate_loc, n_exp, capacity)
-        slots = slots.reshape(expert_ranks, local_exp, tok_loc)
-        gates = gates.reshape(expert_ranks, local_exp, tok_loc)
         any_spec = pl.BlockSpec(memory_space=pl.ANY)
         vmem_spec = pl.BlockSpec(memory_space=pltpu.VMEM)
         dma = pltpu.SemaphoreType.DMA
@@ -354,20 +553,27 @@
                 jax.ShapeDtypeStruct((local_exp, 3, ffn, d_model), BF16),
                 jax.ShapeDtypeStruct((local_exp, expert_ranks, capacity, d_model), BF16),
             ),
-            in_specs=[any_spec] * 4 + [vmem_spec] * 3,
+            in_specs=[any_spec] * 4 + [vmem_spec] * 2,
             out_specs=(vmem_spec, any_spec, any_spec),
             scratch_shapes=[
                 pltpu.VMEM((RING, RING, tok_loc, d_model), BF16),
                 pltpu.VMEM((expert_ranks, local_exp, tok_loc), F32),
+                pltpu.VMEM((expert_ranks, local_exp, tok_loc), F32),
+                pltpu.VMEM((local_exp, expert_ranks, tok_loc), F32),
+                pltpu.VMEM((local_exp, expert_ranks, tok_loc), F32),
                 pltpu.VMEM((local_exp, n_rows, d_model), BF16),
                 pltpu.VMEM((3, ffn, d_model), BF16),
                 pltpu.VMEM((2, n_rows, d_model), BF16),
                 pltpu.VMEM((expert_ranks, capacity, d_model), BF16),
                 pltpu.VMEM((tok_loc, d_model), F32),
-                dma((2, 3, local_exp)),
-                dma((2, 3, local_exp)),
-                dma((7, local_exp)),
-                dma((7, local_exp)),
+                dma((2, 3, local_exp - 2)),
+                dma((2, 3, local_exp - 2)),
+                dma((7, local_exp - 2)),
+                dma((7, local_exp - 2)),
+                dma((2, 3, 5 + BLOCKS)),
+                dma((2, 3, 5 + BLOCKS)),
+                dma((7, 5 + BLOCKS)),
+                dma((7, 5 + BLOCKS)),
                 dma((4, 3)),
                 dma((4, 3)),
                 dma((4, 3)),
@@ -376,9 +582,13 @@
                 dma((expert_ranks,)),
                 dma((2, expert_ranks)),
                 dma((local_exp, expert_ranks)),
-                dma((10,)),
+                dma((BLOCKS, expert_ranks)),
+                dma((BLOCKS, expert_ranks)),
+                dma((5 + BLOCKS, 8)),
                 dma((2,)),
+                dma((BLOCKS,)),
                 dma,
+                dma((BLOCKS,)),
                 dma,
             ],
             compiler_params=pltpu.CompilerParams(collective_id=0, has_side_effects=True, vmem_limit_bytes=67000000),
@@ -387,9 +597,8 @@
             jnp.swapaxes(wg_loc, 1, 2),
             jnp.swapaxes(wu_loc, 1, 2),
             wd_loc,
-            slots,
-            jnp.swapaxes(slots, 0, 1),
-            jnp.swapaxes(gates, 0, 1),
+            ids_loc.T,
+            gate_loc.T,
         )
         return out[0]
 

time: 387 us -> 366 us (0.946)
  Pallas kernels: 380 us -> 361 us
    pallas_call x1, Pallas kernels: 380 us -> 361 us  [local_layer(): pl.pallas_call(functools.partial(moe_kernel, expert_ranks, local_exp, cap...]
where the time goes in v3:
time: 366 us; the launch traced here: 363 us
  Pallas kernels  361 us (99%)
    pallas_call x1, Pallas kernels, local_layer(): pl.pallas_call(functools.partial(moe_kernel, expert_ranks, local_exp, cap...  361 us

profile of v3, /device:TPU:1, one launch (start us, length us, event | category | flops | bytes accessed | tf_op | source)
XLA Modules:
  0.0 363.2 jit_solution(15371727370226658191)
XLA Ops:
  0.0 360.9 %shard_map.64 = (bf16[256,2048]{1,0:T(8,128)(2,1)}, bf16[8,3,768,2048]{3,2,1,0:T(8,128)(2,1)}, bf16[8,16,32,2048]{3,2,1,0:T(8,128)(2,1)}) custom-call(bf16[256,2048]{1,0:T(8,128)(2,1)} %x_hbm.1, bf16[8,96,2048]{2,1,0:T(8,128)(2,1)} %bitcast.4, bf16[8,96,2048]{2,1,0:T(8,128)(2,1)} %bitcast.5, bf16[8,96,2048]{2,1,0:T(8,128)(2,1)} %wd.1, s32[8,256]{1,0:T(8,128)} %bitcast.6, ...), custom_call_target="tpu_custom_call" | custom-call | tf_op jit(solution)/shard_map/pallas_call | solution.py:549
  360.9 2.3 copy.8

commit v4 on v3

--- a/solution.py
+++ b/solution.py
@@ -23,7 +23,7 @@
     return pltpu.make_async_remote_copy(src_ref=src, dst_ref=dst, send_sem=send, recv_sem=recv, device_id=device, device_id_type=MESH)
 
 
-def moe_kernel(n_rank, n_loc, capacity, x_hbm, wg, wu, wd, ids, gate_vals, out, wfull, yret, tok, meta, slots_send, slots_own, gates_own, rows_in, wbuf, ybuf, retbuf, acc, ring_s, ring_r, part_s, part_r, fine_s, fine_r, fpart_s, fpart_r, line_s, line_r, plane_s, plane_r, meta_s, meta_r, y_s, y_r, yb_s, yb_r, load_sem, own_sem, ownb_sem, ret_sem, retb_sem, tok_sem):
+def moe_kernel(n_rank, n_loc, capacity, x_hbm, wg, wu, wd, ids, gate_vals, out, wfull, yret, tok, meta, slots_send, slots_own, gates_own, rows_in, wbuf, wlast, ybuf, retbuf, retlast, hid, acc, ring_s, ring_r, part_s, part_r, fine_s, fine_r, fpart_s, fpart_r, line_s, line_r, plane_s, plane_r, meta_s, meta_r, y_s, y_r, yb_s, yb_r, load_sem, last_sem, own_sem, ret_sem, out_sem, tok_sem):
     ep = lax.axis_index("ep")
     tp = lax.axis_index("tp")
     z, y = ep // RING, lax.rem(ep, RING)
@@ -81,6 +81,7 @@
 
     coarse = n_loc - 2
     width = x_hbm.shape[1] // BLOCKS
+    third = wbuf.shape[1] // 3
     parts6 = (0, 1, 2)
     parts7 = (3, 4)
     down7 = tuple(range(5, 5 + BLOCKS))
@@ -98,7 +99,7 @@
 
     def fine_land(q, rows):
         e, i, c = fine_at(q)
-        return wfull.at[e, i, rows, c]
+        return wfull.at[e, i, rows, c] if q < 3 else wlast.at[i, rows, c]
 
     def fine_start(d, s, q):
         if s == 0:
@@ -140,11 +141,17 @@
             for d in range(2):
                 fine_share(d, s, q)
 
-    def fine_load(q):
+    def fine_shared(q):
         fine_share_own_desc(q).wait_recv()
         for d in range(2):
             for s in range(3):
                 fine_share_desc(d, s, q).wait_recv()
+
+    def last_own(i):
+        return pltpu.make_async_copy(weights[i].at[coarse + 1], wlast.at[i, own_rows(tp), :], last_sem.at[i])
+
+    def fine_load(q):
+        fine_shared(q)
         e, i, c = fine_at(q)
         copies = [pltpu.make_async_copy(fine_own(q, pl.ds(0, cols)), wbuf.at[i, own_rows(tp), c], load_sem.at[q, 0])]
         for j in range(1, RING * CORES):
@@ -218,16 +225,12 @@
 
     def yb_send(n, j):
         r, c = peer(j), pl.ds(n * width, width)
-        return remote(ybuf.at[1, src_rows(r), c], yret.at[n_loc - 1, ep, :, c], yb_s.at[n, j], yb_r.at[n, j], ep=r)
+        return remote(ybuf.at[1, src_rows(r), c], retlast.at[ep, :, c], yb_s.at[n, j], yb_r.at[n, j], ep=r)
 
     def yb_recv(n, j):
         r, c = back_peer(j), pl.ds(n * width, width)
-        piece = yret.at[n_loc - 1, r, :, c]
+        piece = retlast.at[r, :, c]
         return remote(piece, piece, yb_s.at[n, j], yb_r.at[n, j], ep=peer(j))
-
-    def yb_own(n):
-        c = pl.ds(n * width, width)
-        return pltpu.make_async_copy(ybuf.at[1, src_rows(ep), c], yret.at[n_loc - 1, ep, :, c], ownb_sem.at[n])
 
     barrier = pltpu.get_barrier_semaphore()
     for j in range(1, n_rank):
@@ -236,48 +239,24 @@
         pl.semaphore_signal(barrier, inc=1, device_id={"tp": t}, device_id_type=MESH)
     pl.semaphore_wait(barrier, n_rank - 1 + 3)
 
-    def ring_issue(b, static):
-        def when(cond, fn):
-            if static:
-                if cond:
-                    fn()
-            else:
-                pl.when(cond)(fn)
-
-        def first():
+    def send_first(e):
+        for d in range(2):
+            ring_start(d, 0, e)
+        share_own(e)
+
+    def forward(s, e):
+        for d in range(2):
+            ring_desc(d, s, e).wait_recv()
+            ring_start(d, s + 1, e)
+        for d in range(2):
+            share(d, s, e)
+
+    def fine_first(items):
+        for q in items:
             for d in range(2):
-                ring_desc(d, 0, b).wait_recv()
-                ring_start(d, 1, b)
-            for d in range(2):
-                share(d, 0, b)
-
-        def second():
-            for d in range(2):
-                ring_desc(d, 1, b - 1).wait_recv()
-                ring_start(d, 2, b - 1)
-            for d in range(2):
-                share(d, 1, b - 1)
-
-        def ahead():
-            for d in range(2):
-                ring_start(d, 0, b + 2)
-            share_own(b + 2)
-
-        def ahead_fine():
-            for q in parts6:
-                for d in range(2):
-                    fine_start(d, 0, q)
-            for q in parts6:
-                fine_share_own(q)
-
-        first()
-        if static:
-            if 1 <= b:
-                second()
-        else:
-            second()
-        when(b + 2 < coarse, ahead)
-        when(b + 2 == coarse, ahead_fine)
+                fine_start(d, 0, q)
+        for q in items:
+            fine_share_own(q)
 
     def mix_parts(e):
         slot_iota = lax.broadcasted_iota(jnp.int32, (n_rank, capacity, tok_loc), 1).astype(F32)
@@ -306,20 +285,27 @@
             blk = pl.ds(n * width, width)
             acc[:, blk] += mixed(parts, retbuf[:, :, blk])
 
-    def hidden_of(e):
+    def hidden_third(e, w, f):
+        blk = pl.ds(pl.multiple_of(f * third, third) if not isinstance(f, int) else f * third, third)
+        dims = (((1,), (1,)), ((), ()))
         xe = rows_in[e]
-        hidden = []
-        for f in range(3):
-            blk = pl.ds(f * 256, 256)
-            dims = (((1,), (1,)), ((), ()))
-            a = lax.dot_general(xe, wbuf[0, blk, :], dims, preferred_element_type=F32)
-            b = lax.dot_general(xe, wbuf[1, blk, :], dims, preferred_element_type=F32)
-            hidden.append((jax.nn.silu(a) * b).astype(BF16))
-        return jnp.concatenate(hidden, axis=1)
-
-    def down(h, k, n):
-        blk = pl.ds(n * width, width)
-        ybuf[k, :, blk] = jnp.dot(h, wbuf[2, :, blk], preferred_element_type=F32).astype(BF16)
+        a = lax.dot_general(xe, w[0, blk, :], dims, preferred_element_type=F32)
+        b = lax.dot_general(xe, w[1, blk, :], dims, preferred_element_type=F32)
+        hid[:, blk] = (jax.nn.silu(a) * b).astype(BF16)
+
+    def hidden_of(e, w):
+        @pl.loop(0, 3)
+        def _(f):
+            hidden_third(e, w, f)
+
+    def down(k, w, n):
+        blk = pl.ds(pl.multiple_of(n * width, width) if not isinstance(n, int) else n * width, width)
+        ybuf[k, :, blk] = jnp.dot(hid[...], w[2, :, blk], preferred_element_type=F32).astype(BF16)
+
+    def down_all(k, w):
+        @pl.loop(0, BLOCKS)
+        def _(n):
+            down(k, w, n)
 
     def expert(e):
         for d in range(2):
@@ -350,9 +336,8 @@
 
         for c in copies:
             c.wait()
-        h = hidden_of(e)
-        for n in range(BLOCKS):
-            down(h, k, n)
+        hidden_of(e, wbuf)
+        down_all(k, wbuf)
         y_own(e, k).start()
         for j in range(1, n_rank):
             y_send(e, k, j).start()
@@ -387,6 +372,8 @@
     slots_own[...] = slots.reshape(slots_own.shape)
     gates_own[...] = gates.reshape(gates_own.shape)
     acc[...] = jnp.zeros_like(acc)
+    for i in range(3):
+        last_own(i).start()
     for s in range(2):
         for q in range(4):
             line_desc(q, s).wait_recv()
@@ -395,17 +382,21 @@
             for j in range(1, n_rank):
                 remote(slots_send.at[peer(j)], meta.at[ep], meta_s.at[j], meta_r.at[j], ep=peer(j)).start()
             meta[ep] = slots_send[ep]
-    ring_issue(0, True)
+    forward(0, 0)
     load_own.wait()
     for q in range(4):
         line_desc(q, 2).wait_recv()
     for q in range(4):
         plane_start(q, 0)
-    ring_issue(1, True)
+    forward(0, 1)
+    send_first(2)
+    forward(1, 0)
     for q in range(4):
         plane_desc(q, 0).wait_recv()
         plane_start(q, 1)
-    ring_issue(2, True)
+    forward(1, 1)
+    forward(0, 2)
+    send_first(3)
     for q in range(4):
         plane_desc(q, 1).wait_recv()
         plane_start(q, 2)
@@ -422,34 +413,47 @@
         for e in range(n_loc):
             rows_in[e, src_rows(s), :] = picked[e * capacity:(e + 1) * capacity]
 
-    @pl.loop(2, coarse)
+    forward(1, 2)
+
+    @pl.loop(0, coarse - 2)
     def _(b):
-        @pl.when(b > 2)
+        expert(b)
+
+        @pl.when(b == 0)
         def _():
-            ring_issue(b, False)
-
-        expert(b - 2)
-
-        @pl.when(b > 2)
+            forward(0, 3)
+            send_first(4)
+
+        @pl.when(b >= 2)
         def _():
-            combine(b - 3)
-
-    for d in range(2):
-        ring_desc(d, 1, coarse - 1).wait_recv()
-        ring_start(d, 2, coarse - 1)
-        share(d, 1, coarse - 1)
+            forward(1, b + 1)
+
+        @pl.when(b >= 1)
+        def _():
+            combine(b - 1)
+
+        @pl.when(b >= 2)
+        def _():
+            forward(0, b + 2)
+
+        @pl.when(b == 2)
+        def _():
+            send_first(5)
+
+        @pl.when(b == 3)
+        def _():
+            fine_first(parts6)
+
+    expert(coarse - 2)
+    forward(1, coarse - 1)
+    combine(coarse - 3)
     fine_forward(0, parts6)
+    fine_first(parts7[:1])
     fine_share_all(0, parts6)
-    expert(coarse - 2)
-    combine(coarse - 3)
     expert(coarse - 1)
     fine_forward(1, parts6)
-    for q in parts7 + down7:
-        for d in range(2):
-            fine_start(d, 0, q)
+    fine_first(parts7[1:] + down7)
     fine_share_all(1, parts6)
-    for q in parts7 + down7:
-        fine_share_own(q)
     combine(coarse - 2)
 
     fine_forward(2, parts6)
@@ -457,15 +461,14 @@
     for c in loads:
         c.wait()
     loads = fine_load(2)
-    h = hidden_of(coarse)
+    hidden_of(coarse, wbuf)
     fine_forward(0, parts7)
     fine_share_all(0, parts7)
     for j in range(1, n_rank):
         y_send(coarse - 2, 0, j).wait_send()
     for c in loads:
         c.wait()
-    for n in range(BLOCKS):
-        down(h, 0, n)
+    down_all(0, wbuf)
     y_own(coarse, 0).start()
     for j in range(1, n_rank):
         y_send(coarse, 0, j).start()
@@ -475,40 +478,55 @@
     fine_share_all(1, parts7)
     fine_share_all(0, down7)
     combine(coarse - 1)
+    for j in range(1, n_rank):
+        y_send(coarse - 1, 1, j).wait_send()
+    for i in range(3):
+        last_own(i).wait()
     fine_forward(2, parts7)
-    fine_forward(1, down7)
+    for q in parts7:
+        fine_shared(q)
+    last = coarse + 1
+    hidden_third(last, wlast, 0)
+    fine_forward(1, down7[:2])
+    hidden_third(last, wlast, 1)
+    fine_forward(1, down7[2:])
     fine_share_all(1, down7)
-    loads = fine_load(3) + fine_load(4)
-    for c in loads:
-        c.wait()
-    h = hidden_of(coarse + 1)
-    for j in range(1, n_rank):
-        y_send(coarse - 1, 1, j).wait_send()
-    fine_forward(2, down7)
-    block_loads = [fine_load(q) for q in down7]
-    for n in range(BLOCKS):
-        for c in block_loads[n]:
-            c.wait()
-        down(h, 1, n)
-        yb_own(n).start()
+    hidden_third(last, wlast, 2)
+
+    def last_block(n):
+        fine_shared(down7[n])
+        down(1, wlast, n)
         for j in range(1, n_rank):
             yb_send(n, j).start()
+        blk = pl.ds(n * width, width)
+        retlast[ep, :, blk] = ybuf[1, src_rows(ep), blk]
+
+    fine_forward(2, down7[:1])
+    for n in range(1, BLOCKS):
+        fine_forward(2, down7[n:n + 1])
+        last_block(n - 1)
+    last_block(BLOCKS - 1)
     combine(coarse)
-    parts = mix_parts(coarse + 1)
+    parts = mix_parts(last)
+    for j in range(1, n_rank):
+        y_send(coarse, 0, j).wait_send()
+
+    def out_copy(n):
+        blk = pl.ds(n * width, width)
+        return pltpu.make_async_copy(ybuf.at[0, pl.ds(0, tok_loc), blk], out.at[:, blk], out_sem.at[n])
+
     for n in range(BLOCKS):
         blk = pl.ds(n * width, width)
         for j in range(1, n_rank):
             yb_recv(n, j).wait_recv()
-        yb_own(n).wait()
-        load = pltpu.make_async_copy(yret.at[coarse + 1, :, :, blk], retbuf.at[:, :, blk], retb_sem.at[n])
-        load.start()
-        load.wait()
-        out[:, blk] = (acc[:, blk] + mixed(parts, retbuf[:, :, blk])).astype(out.dtype)
-
-    for j in range(1, n_rank):
-        y_send(coarse, 0, j).wait_send()
+        ybuf[0, pl.ds(0, tok_loc), blk] = (acc[:, blk] + mixed(parts, retlast[:, :, blk])).astype(out.dtype)
+        out_copy(n).start()
+
+    for j in range(1, n_rank):
         for n in range(BLOCKS):
             yb_send(n, j).wait_send()
+    for n in range(BLOCKS):
+        out_copy(n).wait()
     for q in range(5 + BLOCKS):
         fine_share_own_desc(q).wait_send()
         for d in range(2):
@@ -550,11 +568,11 @@
             functools.partial(moe_kernel, expert_ranks, local_exp, capacity),
             out_shape=(
                 jax.ShapeDtypeStruct((tok_loc, d_model), BF16),
-                jax.ShapeDtypeStruct((local_exp, 3, ffn, d_model), BF16),
-                jax.ShapeDtypeStruct((local_exp, expert_ranks, capacity, d_model), BF16),
+                jax.ShapeDtypeStruct((local_exp - 1, 3, ffn, d_model), BF16),
+                jax.ShapeDtypeStruct((local_exp - 1, expert_ranks, capacity, d_model), BF16),
             ),
             in_specs=[any_spec] * 4 + [vmem_spec] * 2,
-            out_specs=(vmem_spec, any_spec, any_spec),
+            out_specs=(any_spec, any_spec, any_spec),
             scratch_shapes=[
                 pltpu.VMEM((RING, RING, tok_loc, d_model), BF16),
                 pltpu.VMEM((expert_ranks, local_exp, tok_loc), F32),
@@ -563,8 +581,11 @@
                 pltpu.VMEM((local_exp, expert_ranks, tok_loc), F32),
                 pltpu.VMEM((local_exp, n_rows, d_model), BF16),
                 pltpu.VMEM((3, ffn, d_model), BF16),
+                pltpu.VMEM((3, ffn, d_model), BF16),
                 pltpu.VMEM((2, n_rows, d_model), BF16),
                 pltpu.VMEM((expert_ranks, capacity, d_model), BF16),
+                pltpu.VMEM((expert_ranks, capacity, d_model), BF16),
+                pltpu.VMEM((n_rows, ffn), BF16),
                 pltpu.VMEM((tok_loc, d_model), F32),
                 dma((2, 3, local_exp - 2)),
                 dma((2, 3, local_exp - 2)),
@@ -584,9 +605,9 @@
                 dma((local_exp, expert_ranks)),
                 dma((BLOCKS, expert_ranks)),
                 dma((BLOCKS, expert_ranks)),
-                dma((5 + BLOCKS, 8)),
+                dma((3, 8)),
+                dma((3,)),
                 dma((2,)),
-                dma((BLOCKS,)),
                 dma,
                 dma((BLOCKS,)),
                 dma,

time: 366 us -> 365 us (level)
  no operation moved by 1% of the time
where the time goes in v4:
time: 365 us; the launch traced here: 364 us
  Pallas kernels  362 us (99%)
    pallas_call x1, Pallas kernels, local_layer(): pl.pallas_call(functools.partial(moe_kernel, expert_ranks, local_exp, cap...  362 us

profile of v4, /device:TPU:1, one launch (start us, length us, event | category | flops | bytes accessed | tf_op | source)
XLA Modules:
  0.0 364.0 jit_solution(46140062380424574)
XLA Ops:
  0.0 361.7 %shard_map.64 = (bf16[256,2048]{1,0:T(8,128)(2,1)}, bf16[7,3,768,2048]{3,2,1,0:T(8,128)(2,1)}, bf16[7,16,32,2048]{3,2,1,0:T(8,128)(2,1)}) custom-call(bf16[256,2048]{1,0:T(8,128)(2,1)} %x_hbm.1, bf16[8,96,2048]{2,1,0:T(8,128)(2,1)} %bitcast.4, bf16[8,96,2048]{2,1,0:T(8,128)(2,1)} %bitcast.5, bf16[8,96,2048]{2,1,0:T(8,128)(2,1)} %wd.1, s32[8,256]{1,0:T(8,128)} %bitcast.6, ...), custom_call_target="tpu_custom_call" | custom-call | tf_op jit(solution)/shard_map/pallas_call | solution.py:567
  361.7 2.3 copy.8

commit v5 on v4

--- a/solution.py
+++ b/solution.py
@@ -239,24 +239,48 @@
         pl.semaphore_signal(barrier, inc=1, device_id={"tp": t}, device_id_type=MESH)
     pl.semaphore_wait(barrier, n_rank - 1 + 3)
 
-    def send_first(e):
-        for d in range(2):
-            ring_start(d, 0, e)
-        share_own(e)
-
-    def forward(s, e):
-        for d in range(2):
-            ring_desc(d, s, e).wait_recv()
-            ring_start(d, s + 1, e)
-        for d in range(2):
-            share(d, s, e)
-
-    def fine_first(items):
-        for q in items:
+    def ring_issue(b, static):
+        def when(cond, fn):
+            if static:
+                if cond:
+                    fn()
+            else:
+                pl.when(cond)(fn)
+
+        def first():
             for d in range(2):
-                fine_start(d, 0, q)
-        for q in items:
-            fine_share_own(q)
+                ring_desc(d, 0, b).wait_recv()
+                ring_start(d, 1, b)
+            for d in range(2):
+                share(d, 0, b)
+
+        def second():
+            for d in range(2):
+                ring_desc(d, 1, b - 1).wait_recv()
+                ring_start(d, 2, b - 1)
+            for d in range(2):
+                share(d, 1, b - 1)
+
+        def ahead():
+            for d in range(2):
+                ring_start(d, 0, b + 2)
+            share_own(b + 2)
+
+        def ahead_fine():
+            for q in parts6:
+                for d in range(2):
+                    fine_start(d, 0, q)
+            for q in parts6:
+                fine_share_own(q)
+
+        first()
+        if static:
+            if 1 <= b:
+                second()
+        else:
+            second()
+        when(b + 2 < coarse, ahead)
+        when(b + 2 == coarse, ahead_fine)
 
     def mix_parts(e):
         slot_iota = lax.broadcasted_iota(jnp.int32, (n_rank, capacity, tok_loc), 1).astype(F32)
@@ -307,7 +331,7 @@
         def _(n):
             down(k, w, n)
 
-    def expert(e):
+    def expert(e, before_hidden=None, before_down=None):
         for d in range(2):
             ring_desc(d, 2, e).wait_recv()
             share(d, 2, e)
@@ -336,7 +360,11 @@
 
         for c in copies:
             c.wait()
+        if before_hidden is not None:
+            before_hidden()
         hidden_of(e, wbuf)
+        if before_down is not None:
+            before_down()
         down_all(k, wbuf)
         y_own(e, k).start()
         for j in range(1, n_rank):
@@ -382,21 +410,17 @@
             for j in range(1, n_rank):
                 remote(slots_send.at[peer(j)], meta.at[ep], meta_s.at[j], meta_r.at[j], ep=peer(j)).start()
             meta[ep] = slots_send[ep]
-    forward(0, 0)
+    ring_issue(0, True)
     load_own.wait()
     for q in range(4):
         line_desc(q, 2).wait_recv()
     for q in range(4):
         plane_start(q, 0)
-    forward(0, 1)
-    send_first(2)
-    forward(1, 0)
+    ring_issue(1, True)
     for q in range(4):
         plane_desc(q, 0).wait_recv()
         plane_start(q, 1)
-    forward(1, 1)
-    forward(0, 2)
-    send_first(3)
+    ring_issue(2, True)
     for q in range(4):
         plane_desc(q, 1).wait_recv()
         plane_start(q, 2)
@@ -413,47 +437,34 @@
         for e in range(n_loc):
             rows_in[e, src_rows(s), :] = picked[e * capacity:(e + 1) * capacity]
 
-    forward(1, 2)
-
-    @pl.loop(0, coarse - 2)
+    @pl.loop(2, coarse)
     def _(b):
-        expert(b)
-
-        @pl.when(b == 0)
+        @pl.when(b > 2)
         def _():
-            forward(0, 3)
-            send_first(4)
-
-        @pl.when(b >= 2)
+            ring_issue(b, False)
+
+        expert(b - 2)
+
+        @pl.when(b > 2)
         def _():
-            forward(1, b + 1)
-
-        @pl.when(b >= 1)
-        def _():
-            combine(b - 1)
-
-        @pl.when(b >= 2)
-        def _():
-            forward(0, b + 2)
-
-        @pl.when(b == 2)
-        def _():
-            send_first(5)
-
-        @pl.when(b == 3)
-        def _():
-            fine_first(parts6)
-
+            combine(b - 3)
+
+    for d in range(2):
+        ring_desc(d, 1, coarse - 1).wait_recv()
+        ring_start(d, 2, coarse - 1)
+        share(d, 1, coarse - 1)
+    fine_forward(0, parts6)
+    fine_share_all(0, parts6)
     expert(coarse - 2)
-    forward(1, coarse - 1)
     combine(coarse - 3)
-    fine_forward(0, parts6)
-    fine_first(parts7[:1])
-    fine_share_all(0, parts6)
-    expert(coarse - 1)
-    fine_forward(1, parts6)
-    fine_first(parts7[1:] + down7)
+    expert(coarse - 1, lambda: fine_forward(1, parts6[:1]), lambda: fine_forward(1, parts6[1:2]))
+    fine_forward(1, parts6[2:])
+    for q in parts7 + down7:
+        for d in range(2):
+            fine_start(d, 0, q)
     fine_share_all(1, parts6)
+    for q in parts7 + down7:
+        fine_share_own(q)
     combine(coarse - 2)
 
     fine_forward(2, parts6)

time: 365 us -> 362 us (level)
  no operation moved by 1% of the time
where the time goes in v5:
time: 362 us
  Pallas kernels  360 us (99%)
    pallas_call x1, Pallas kernels, local_layer(): pl.pallas_call(functools.partial(moe_kernel, expert_ranks, local_exp, cap...  360 us

profile of v5, /device:TPU:1, one launch (start us, length us, event | category | flops | bytes accessed | tf_op | source)
XLA Modules:
  0.0 361.9 jit_solution(16817236762862941927)
XLA Ops:
  0.0 359.6 %shard_map.64 = (bf16[256,2048]{1,0:T(8,128)(2,1)}, bf16[7,3,768,2048]{3,2,1,0:T(8,128)(2,1)}, bf16[7,16,32,2048]{3,2,1,0:T(8,128)(2,1)}) custom-call(bf16[256,2048]{1,0:T(8,128)(2,1)} %x_hbm.1, bf16[8,96,2048]{2,1,0:T(8,128)(2,1)} %bitcast.4, bf16[8,96,2048]{2,1,0:T(8,128)(2,1)} %bitcast.5, bf16[8,96,2048]{2,1,0:T(8,128)(2,1)} %wd.1, s32[8,256]{1,0:T(8,128)} %bitcast.6, ...), custom_call_target="tpu_custom_call" | custom-call | tf_op jit(solution)/shard_map/pallas_call | solution.py:578
  359.6 2.3 copy.8

commit v6 on v4

--- a/solution.py
+++ b/solution.py
@@ -307,7 +307,7 @@
         def _(n):
             down(k, w, n)
 
-    def expert(e):
+    def expert(e, before_hidden=None, before_down=None):
         for d in range(2):
             ring_desc(d, 2, e).wait_recv()
             share(d, 2, e)
@@ -336,7 +336,11 @@
 
         for c in copies:
             c.wait()
+        if before_hidden is not None:
+            before_hidden()
         hidden_of(e, wbuf)
+        if before_down is not None:
+            before_down()
         down_all(k, wbuf)
         y_own(e, k).start()
         for j in range(1, n_rank):
@@ -448,11 +452,10 @@
     forward(1, coarse - 1)
     combine(coarse - 3)
     fine_forward(0, parts6)
-    fine_first(parts7[:1])
     fine_share_all(0, parts6)
-    expert(coarse - 1)
-    fine_forward(1, parts6)
-    fine_first(parts7[1:] + down7)
+    expert(coarse - 1, lambda: fine_forward(1, parts6[:1]), lambda: fine_forward(1, parts6[1:2]))
+    fine_forward(1, parts6[2:])
+    fine_first(parts7 + down7)
     fine_share_all(1, parts6)
     combine(coarse - 2)
 

time: 365 us -> 364 us (level)
  no operation moved by 1% of the time
where the time goes in v6:
time: 364 us; the launch traced here: 361 us
  Pallas kernels  359 us (99%)
    pallas_call x1, Pallas kernels, local_layer(): pl.pallas_call(functools.partial(moe_kernel, expert_ranks, local_exp, cap...  359 us

profile of v6, /device:TPU:1, one launch (start us, length us, event | category | flops | bytes accessed | tf_op | source)
XLA Modules:
  0.0 361.1 jit_solution(3516183899927703268)
XLA Ops:
  0.0 358.8 %shard_map.64 = (bf16[256,2048]{1,0:T(8,128)(2,1)}, bf16[7,3,768,2048]{3,2,1,0:T(8,128)(2,1)}, bf16[7,16,32,2048]{3,2,1,0:T(8,128)(2,1)}) custom-call(bf16[256,2048]{1,0:T(8,128)(2,1)} %x_hbm.1, bf16[8,96,2048]{2,1,0:T(8,128)(2,1)} %bitcast.4, bf16[8,96,2048]{2,1,0:T(8,128)(2,1)} %bitcast.5, bf16[8,96,2048]{2,1,0:T(8,128)(2,1)} %wd.1, s32[8,256]{1,0:T(8,128)} %bitcast.6, ...), custom_call_target="tpu_custom_call" | custom-call | tf_op jit(solution)/shard_map/pallas_call | solution.py:570
  358.8 2.3 copy.8
